TPU v7x, 32 devices: a whole 2x2x4 slice. The times are simulated.
32 devices in a mesh: row: 8 (over z, x), col: 4 (over y, core).
Axes of the slice: x: 2, y: 2, z: 4, core: 2. Of those that a mesh axis runs over, the one named last changes fastest.
Arguments:
- queries: bfloat16 [8192, 2048], P(('row', 'col')), may hold values from -200 to 200
- keys: bfloat16 [8192, 512], P(('row', 'col')), may hold values from -6 to 6
- values: bfloat16 [8192, 512], P(('row', 'col')), may hold values from -6 to 6
- mid_key_weight: bfloat16 [1024, 128], replicated, may hold values from -0.1875 to 0.1875
- mid_value_weight: bfloat16 [1024, 128], replicated, may hold values from -0.1875 to 0.1875
- far_key_weight: bfloat16 [2048, 128], replicated, may hold values from -0.125 to 0.125
- far_value_weight: bfloat16 [2048, 128], replicated, may hold values from -0.125 to 0.125
Outputs:
- attended: bfloat16 [8192, 2048], P(('row', 'col'))
All inputs are finite; a program needn't handle non-finite values.
Results may differ from a plain program's by a relative error of at most 0.012.
Values may be sent and summed in bfloat16 or wider, within the bound.
A program may use at most 128 MiB of HBM per device.

v0:
```python
import functools
import math

import jax
import jax.numpy as jnp
from jax import lax
from jax.experimental import pallas as pl
from jax.experimental.pallas import tpu as pltpu
from jax.sharding import PartitionSpec as P

HQ = 16
HK = 4
DH = 128
BLOCK = 512
MID = 8
FAR = 16
GROUP = HQ // HK
KV = HK * DH
NEG_FILL = -1e30
EXP_SCALE = DH ** (-0.5) * math.log2(math.e)
FAR_CHUNK = 512
VMEM_LIMIT = 57 * 1024 * 1024
MESH = pl.DeviceIdType.MESH
FROM_PARTNER, FROM_BEHIND, RELAYED = 0, 1, 2


def score(q, k):
    return lax.dot_general(q, k, (((1,), (1,)), ((), ())), preferred_element_type=jnp.float32)


def weigh(p, v):
    both = jnp.concatenate([v, jnp.ones_like(v)], axis=1)
    return jnp.dot(p.astype(jnp.bfloat16), both, preferred_element_type=jnp.float32)


def powers(s, top):
    return jnp.exp2((s - top) * EXP_SCALE)


def normalised(acc):
    return acc[:, :DH] / jnp.maximum(acc[:, DH:], 1.0)


def kernel(
    rows, cols,
    q_hbm, k_hbm, v_hbm, wmk_hbm, wmv_hbm, wfk_hbm, wfv_hbm, out_ref,
    q_ref, k_ref, v_ref, wmk_ref, wmv_ref, wfk_ref, wfv_ref, fetch_sem,
    wide, mid_buf, far_own, far_buf, near, top_ref, acc_ref, rest_ref,
    near_send, near_recv, mid_send, mid_recv,
    f1_send, f1_recv, f2_send, f2_recv, f3_send, f3_recv,
):
    tok = q_ref.shape[0]
    mids, fars = tok // MID, tok // FAR
    total = rows * cols
    pairs = cols // 2
    row, col = lax.axis_index("row"), lax.axis_index("col")
    pos = row * cols + col
    side = lax.rem(col, 2)
    pair = col // 2
    other = col + 1 - 2 * side
    partner = (row, other)

    def fetch(i, src, dst):
        return pltpu.make_async_copy(src, dst, fetch_sem.at[i])

    fetches = [
        fetch(i, src, dst)
        for i, (src, dst) in enumerate((
            (k_hbm, k_ref), (wfk_hbm, wfk_ref), (wmk_hbm, wmk_ref),
            (v_hbm, v_ref), (wfv_hbm, wfv_ref), (wmv_hbm, wmv_ref), (q_hbm, q_ref),
        ))
    ]
    for copy in fetches:
        copy.start()

    def at(linear):
        return (linear // cols, lax.rem(linear, cols))

    mid_buf[...] = jnp.zeros_like(mid_buf)

    def clear(c, _):
        far_buf[c] = jnp.zeros(far_buf.shape[1:], far_buf.dtype)
        return 0

    lax.fori_loop(0, cols, clear, 0)

    barrier = pltpu.get_barrier_semaphore()

    def greet(device):
        pl.semaphore_signal(barrier, inc=1, device_id=device, device_id_type=MESH)

    def greet_col(i, _):
        greet((row, lax.rem(col + i, cols)))
        return 0

    def greet_row(i, _):
        greet((lax.rem(row + i, rows), col))
        return 0

    lax.fori_loop(1, cols, greet_col, 0)
    lax.fori_loop(1, rows, greet_row, 0)
    greet(at(lax.rem(pos + 2, total)))
    greet(at(lax.rem(pos + total - 2, total)))


    def head_lanes(h, base=0):
        return pl.ds(pl.multiple_of(base + h * DH, DH), DH)

    def remote(src, dst, send, recv, device):
        return pltpu.make_async_remote_copy(
            src_ref=src, dst_ref=dst, send_sem=send, recv_sem=recv,
            device_id=device, device_id_type=MESH,
        )

    def far_slot(c, r):
        return far_buf.at[c, pl.ds(pl.multiple_of(r * fars, fars), fars), :]

    def far1(r_to, r_from):
        return remote(far_own, far_slot(col, r_from), f1_send.at[r_to], f1_recv.at[r_from], (r_to, col))

    def far2(r, p_to, p_from):
        return remote(
            far_slot(2 * p_from + side, r), far_slot(2 * p_from + side, r),
            f2_send.at[p_to, r], f2_recv.at[p_from, r], (row, 2 * p_to + side),
        )

    def far3(r, p, s):
        return remote(
            far_slot(2 * p + s, r), far_slot(2 * p + s, r),
            f3_send.at[p, r], f3_recv.at[p, r], partner,
        )

    def mid_copy(c_to, c_from):
        span = mid_buf.at[pl.ds(pl.multiple_of(c_from * mids, mids), mids), :]
        return remote(span, span, mid_send.at[c_to], mid_recv.at[c_from], (row, c_to))

    def near_copy(slot, i, src, device):
        return remote(
            src, near.at[slot, i], near_send.at[slot, i, 0], near_recv.at[slot, i, 0], device
        )

    def behind_copy(i, h):
        lanes = head_lanes(h)
        return remote(
            own[i].at[:, lanes], near.at[FROM_BEHIND, i, :, lanes],
            near_send.at[FROM_BEHIND, i, h], near_recv.at[FROM_BEHIND, i, h], ahead,
        )

    def relay_copy(i, h):
        lanes = head_lanes(h)
        return remote(
            near.at[FROM_BEHIND, i, :, lanes], near.at[RELAYED, i, :, lanes],
            near_send.at[RELAYED, i, h], near_recv.at[RELAYED, i, h], partner,
        )

    def behind_start(h):
        for i in range(2):
            behind_copy(i, h).start()

    own = (k_ref, v_ref)
    ahead = at(lax.rem(pos + 2, total))

    def loop(low, high, f):
        def step(i, _):
            f(i)
            return 0

        lax.fori_loop(low, high, step, 0)

    mid_rows = pl.ds(pl.multiple_of(col * mids, mids), mids)

    def summarise(s, src, wm, wf):
        for copy in fetches[4 * s:3 * s + 3]:
            copy.wait()
        for h in range(HK):
            wide[s * HK + h] = src[:, h * DH:(h + 1) * DH].astype(jnp.float32)
        for squeeze, count, weight in ((FAR, fars, wf), (MID, mids, wm)):
            grouped = jnp.concatenate(
                [
                    jnp.concatenate(
                        [wide[s * HK + h, pl.ds(i, count, stride=squeeze), :] for h in range(HK)],
                        axis=0,
                    ).astype(jnp.bfloat16)
                    for i in range(squeeze)
                ],
                axis=1,
            )
            merged = jnp.dot(grouped, weight[...], preferred_element_type=jnp.float32)
            merged = merged.astype(jnp.bfloat16)
            for h in range(HK):
                lanes = slice(s * KV + h * DH, s * KV + (h + 1) * DH)
                piece = merged[h * count:(h + 1) * count]
                if squeeze == FAR:
                    far_own[:, lanes] = piece
                else:
                    mid_buf[mid_rows, lanes] = piece

    summarise(0, k_ref, wmk_ref, wfk_ref)
    fetches[3].wait()
    pl.semaphore_wait(barrier, cols + rows)

    @pl.when(pos + 2 < total)
    def _():
        behind_start(0)

    summarise(1, v_ref, wmv_ref, wfv_ref)

    loop(row + 1, rows, lambda r: far1(r, row).start())
    loop(col + 1, cols, lambda c: mid_copy(c, col).start())

    @pl.when(side == 0)
    def _():
        for i in range(2):
            near_copy(FROM_PARTNER, i, own[i], partner).start()

    @pl.when(pos + 2 < total)
    def _():
        loop(1, HK, behind_start)

    fetches[6].wait()

    def query_of(h):
        q = q_ref[:, pl.ds(pl.multiple_of(h * GROUP * DH, DH), GROUP * DH)]
        return jnp.concatenate([q[:, g * DH:(g + 1) * DH] for g in range(GROUP)], axis=0)

    def queries_of(h):
        base = h * GROUP * DH
        return [
            q_ref[:, pl.ds(pl.multiple_of(base + g * DH, DH), DH)] for g in range(GROUP)
        ]

    def tiled_mask(seen, s):
        lines, keys = seen.shape
        shaped = s.reshape(GROUP, lines, keys)
        return shaped, seen[None]

    def masked(seen, s, fill):
        shaped, seen = tiled_mask(seen, s)
        return jnp.where(seen, shaped, fill).reshape(s.shape)

    def iota(shape, axis):
        return lax.broadcasted_iota(jnp.int32, shape, axis)

    def near_first(with_partner):
        def one(h):
            seen = iota((tok, tok), 1) <= iota((tok, tok), 0)
            key_parts = [k_ref[:, head_lanes(h)]]
            value_parts = [v_ref[:, head_lanes(h)]]
            if with_partner:
                key_parts.append(near[FROM_PARTNER, 0, :, head_lanes(h)])
                value_parts.append(near[FROM_PARTNER, 1, :, head_lanes(h)])
            s = [[score(q, k) for k in key_parts] for q in queries_of(h)]
            for g, parts in enumerate(s):
                parts = [jnp.where(seen, parts[0], NEG_FILL)] + parts[1:]
                top = jnp.max(functools.reduce(jnp.maximum, parts), axis=-1, keepdims=True)
                span = slice(g * tok, (g + 1) * tok)
                terms = [weigh(powers(p, top), v) for p, v in zip(parts, value_parts)]
                acc_ref[h, span] = functools.reduce(jnp.add, terms)
                top_ref[h, span] = top

        loop(0, HK, one)

    @pl.when(side == 0)
    def _():
        near_first(False)

    def pass_on(r):
        far1(r, r).wait_recv()

        def to_pair(p):
            @pl.when(p != pair)
            def _():
                far2(r, p, pair).start()

        loop(0, pairs, to_pair)
        far3(r, pair, side).start()

    def far_pass():
        loop(0, row, pass_on)

    @pl.when(side == 0)
    def _():
        far_pass()

    @pl.when(side == 1)
    def _():
        for i in range(2):
            near_copy(FROM_PARTNER, i, own[i], partner).wait_recv()
        near_first(True)
        far_pass()

    loop(0, col, lambda c: mid_copy(c, c).wait_recv())
    n_mid = mid_buf.shape[0]

    def mid_one(h):
        q = query_of(h)
        seen = (iota((tok, n_mid), 1) * MID + MID - 1) <= (iota((tok, n_mid), 0) + col * tok)
        s = masked(seen, score(q, mid_buf[:, head_lanes(h)]), NEG_FILL)
        top = jnp.max(s, axis=-1, keepdims=True)
        p = masked(seen, powers(s, top), 0.0)
        rest_ref[h] = normalised(weigh(p, mid_buf[:, head_lanes(h, KV)]))

    loop(0, HK // 2, mid_one)

    def pass_partner(r):
        def from_pair(p):
            @pl.when(p != pair)
            def _():
                far2(r, p, p).wait_recv()
                far3(r, p, side).start()

        loop(0, pairs, from_pair)

    loop(0, row, pass_partner)
    loop(HK // 2, HK, mid_one)
    loop(0, row, lambda r: loop(0, pairs, lambda p: far3(r, p, 1 - side).wait_recv()))

    line = far_buf.shape[1]
    per = max(1, min(cols, FAR_CHUNK // line))
    n_chunk = cols // per

    def far_one(h):
        q = query_of(h)
        seen = lax.rem(iota((1, per * line), 1), line) < row * fars

        def part(j, base):
            block = far_buf[pl.ds(j * per, per), :, head_lanes(h, base)]
            return block.reshape(per * line, DH)

        def chunk(j, carry):
            s = jnp.where(seen, score(q, part(j, 0)), NEG_FILL)
            top = jnp.max(s, axis=-1, keepdims=True)
            if carry is None:
                return top, weigh(powers(s, top), part(j, KV))
            before, acc = carry
            top = jnp.maximum(before, top)
            return top, acc * powers(before, top) + weigh(powers(s, top), part(j, KV))

        carry = chunk(0, None)
        if n_chunk > 1:
            carry = lax.fori_loop(1, n_chunk, chunk, carry)
        rest_ref[h] = rest_ref[h] + normalised(carry[1])

    def put(h, g, value):
        lanes = pl.ds(pl.multiple_of((h * GROUP + g) * DH, DH), DH)
        out_ref[:, lanes] = value.astype(out_ref.dtype)

    def arrive(h):
        for i in range(2):
            behind_copy(i, h).wait_recv()
            relay_copy(i, h).start()

    def near_last(h):
        for i in range(2):
            relay_copy(i, h).wait_recv()
        parts = (FROM_BEHIND, RELAYED)
        s = [
            [score(q, near[slot, 0, :, head_lanes(h)]) for slot in parts]
            for q in queries_of(h)
        ]
        for g, pair_s in enumerate(s):
            span = slice(g * tok, (g + 1) * tok)
            before = top_ref[h, span]
            top = jnp.maximum(before, jnp.max(jnp.maximum(*pair_s), axis=-1, keepdims=True))
            acc = acc_ref[h, span] * powers(before, top)
            for slot, part in zip(parts, pair_s):
                acc = acc + weigh(powers(part, top), near[slot, 1, :, head_lanes(h)])
            put(h, g, normalised(acc) + rest_ref[h, span])

    def far_step(h):
        @pl.when(row > 0)
        def _():
            far_one(h)

    lead = HK // 2
    loop(0, lead, far_step)

    @pl.when(pos >= 2)
    def _():
        arrive(0)

    def step(h):
        @pl.when(h + lead < HK)
        def _():
            far_step(h + lead)

        @pl.when((pos >= 2) & (h + 1 < HK))
        def _():
            arrive(h + 1)

        @pl.when(pos >= 2)
        def _():
            near_last(h)

    loop(0, HK, step)

    @pl.when(pos < 2)
    def _():
        def one(h):
            for g in range(GROUP):
                span = slice(g * tok, (g + 1) * tok)
                put(h, g, normalised(acc_ref[h, span]) + rest_ref[h, span])

        loop(0, HK, one)

    loop(row + 1, rows, lambda r: far1(r, row).wait_send())
    loop(col + 1, cols, lambda c: mid_copy(c, col).wait_send())

    def sent(r):
        def one(p):
            far3(r, p, side).wait_send()

            @pl.when(p != pair)
            def _():
                far2(r, p, pair).wait_send()

        loop(0, pairs, one)

    loop(0, row, sent)

    @pl.when(side == 0)
    def _():
        for i in range(2):
            near_copy(FROM_PARTNER, i, own[i], partner).wait_send()

    @pl.when(pos + 2 < total)
    def _():
        for i in range(2):
            loop(0, HK, lambda h, i=i: behind_copy(i, h).wait_send())

    @pl.when(pos >= 2)
    def _():
        for i in range(2):
            loop(0, HK, lambda h, i=i: relay_copy(i, h).wait_send())


def body(rows, cols, queries, keys, values, *weights):
    tok = queries.shape[0]
    assert BLOCK == 2 * tok and cols % 2 == 0
    dma = pltpu.SemaphoreType.DMA
    bf16, f32 = jnp.bfloat16, jnp.float32
    lines = GROUP * tok
    vmem = pl.BlockSpec(memory_space=pltpu.VMEM)
    return pl.pallas_call(
        functools.partial(kernel, rows, cols),
        out_shape=pltpu.VMEM(queries.shape, bf16),
        in_specs=[pl.BlockSpec(memory_space=pltpu.HBM)] * 7,
        out_specs=vmem,
        scratch_shapes=[
            *[pltpu.VMEM(a.shape, a.dtype) for a in (queries, keys, values, *weights)],
            dma((7,)),
            pltpu.VMEM((2 * HK, tok, DH), f32),
            pltpu.VMEM((cols * (tok // MID), 2 * KV), bf16),
            pltpu.VMEM((tok // FAR, 2 * KV), bf16),
            pltpu.VMEM((cols, rows * (tok // FAR), 2 * KV), bf16),
            pltpu.VMEM((3, 2, tok, KV), bf16),
            pltpu.VMEM((HK, lines, 1), f32),
            pltpu.VMEM((HK, lines, 2 * DH), f32),
            pltpu.VMEM((HK, lines, DH), f32),
            dma((3, 2, HK)),
            dma((3, 2, HK)),
            dma((cols,)),
            dma((cols,)),
            dma((rows,)),
            dma((rows,)),
            dma((cols // 2, rows)),
            dma((cols // 2, rows)),
            dma((cols // 2, rows)),
            dma((cols // 2, rows)),
        ],
        compiler_params=pltpu.CompilerParams(
            collective_id=0, has_side_effects=True, vmem_limit_bytes=VMEM_LIMIT
        ),
    )(queries, keys, values, *weights)


def solution(mesh):
    spec = P(("row", "col"), None)
    return jax.shard_map(
        functools.partial(body, mesh.shape["row"], mesh.shape["col"]),
        mesh=mesh,
        in_specs=(spec, spec, spec, P(), P(), P(), P()),
        out_specs=spec,
        check_vma=False,
    )
```

profile of v0, /device:TPU:17, one launch (start us, length us, event | category | flops | bytes accessed | tf_op | source)
XLA Modules:
  0.0 39.2 jit_solution(18261889131966550100)
XLA Ops:
  0.0 38.2 %shard_map.73 = bf16[256,2048]{1,0:T(8,128)(2,1)S(1)} custom-call(bf16[256,2048]{1,0:T(8,128)(2,1)} %q_hbm.1, bf16[256,512]{1,0:T(8,128)(2,1)} %k_hbm.1, bf16[256,512]{1,0:T(8,128)(2,1)} %v_hbm.1, bf16[1024,128]{1,0:T(8,128)(2,1)} %wmk_hbm.1, bf16[1024,128]{1,0:T(8,128)(2,1)} %wmv_hbm.1, bf16[2048,128]{1,0:T(8,128)(2,1)} %wfk_hbm.1, bf16[2048,128]{1,0:T(8,128)(2,1)} %wfv_hbm.1), custom_call_target="tpu_custom_call" | custom-call | tf_op jit(solution)/shard_map/pallas_call | solution.py:444
  38.2 1.0 %copy.9 = bf16[256,2048]{1,0:T(8,128)(2,1)} copy(bf16[256,2048]{1,0:T(8,128)(2,1)S(1)} %shard_map.73) | data formatting | bytes 2097152
where the time goes:
time: 39.3 us; the launch traced here: 39.2 us
  Pallas kernels  38.2 us (97%)
  local copies, waits for them, and re-layouts  0.97 us (2%)
    pallas_call x1, Pallas kernels, body(): pl.pallas_call(functools.partial(kernel, rows, cols), out_shape=pltpu.VME...  38.2 us
    unnamed x1, local copies, waits for them, and re-layouts  0.97 us

commit v1 on v0

v1 whole, which is shorter than its diff:
```python
import functools
import math

import jax
import jax.numpy as jnp
from jax import lax
from jax.experimental import pallas as pl
from jax.experimental.pallas import tpu as pltpu
from jax.sharding import PartitionSpec as P

HQ = 16
HK = 4
DH = 128
BLOCK = 512
MID = 8
FAR = 16
GROUP = HQ // HK
KV = HK * DH
NEG_FILL = -1e30
TOP_FLOOR = -1e29
SUM_ROWS = 16
EXP_SCALE = DH ** (-0.5) * math.log2(math.e)
FAR_CHUNK = 512
VMEM_LIMIT = 57 * 1024 * 1024
MESH = pl.DeviceIdType.MESH
FROM_PARTNER, FROM_BEHIND, RELAYED = 0, 1, 2


def score(k, q):
    return lax.dot_general(k, q, (((1,), (1,)), ((), ())), preferred_element_type=jnp.float32)


def powers(s, top):
    return jnp.exp2((s - top) * EXP_SCALE)


def top_of(parts):
    return functools.reduce(jnp.maximum, [jnp.max(s, axis=0, keepdims=True) for s in parts])


def flat(v):
    return jnp.concatenate([v.T, jnp.ones((SUM_ROWS, v.shape[0]), v.dtype)], axis=0)


def weigh(parts, top, flats):
    terms = [
        jnp.dot(v, powers(s, top).astype(jnp.bfloat16), preferred_element_type=jnp.float32)
        for s, v in zip(parts, flats)
    ]
    both = functools.reduce(jnp.add, terms)
    return both[DH:DH + 1], both[:DH]


def inverse(den):
    return 1.0 / jnp.maximum(den, 1.0)


def kernel(
    rows, cols,
    q_hbm, k_hbm, v_hbm, wmk_hbm, wmv_hbm, wfk_hbm, wfv_hbm, out_ref,
    q_ref, k_ref, v_ref, wmk_ref, wmv_ref, wfk_ref, wfv_ref, fetch_sem,
    wide, mid_buf, far_buf, near, top_ref, den_ref, acc_ref, rest_ref,
    near_send, near_recv, mid_send, mid_recv, pass_send, pass_recv,
    swap_send, swap_recv, side_send, side_recv,
    down_send, down_recv, cross_send, cross_recv, twin_send, twin_recv,
):
    tok = q_ref.shape[0]
    mids, fars = tok // MID, tok // FAR
    total = rows * cols
    pairs = cols // 2
    row, col = lax.axis_index("row"), lax.axis_index("col")
    pos = row * cols + col
    side = lax.rem(col, 2)
    pair = col // 2
    low = lax.rem(row, 2)
    high = row // 2
    other_row = row + 1 - 2 * low
    partner = (row, col + 1 - 2 * side)
    beside = (other_row, col)
    is_leaf = (low == 0) & (pair == 0)
    is_last = high + 1 == rows // 2

    def fetch(i, src, dst):
        return pltpu.make_async_copy(src, dst, fetch_sem.at[i])

    fetches = [
        fetch(i, src, dst)
        for i, (src, dst) in enumerate((
            (k_hbm, k_ref), (wfk_hbm, wfk_ref), (wmk_hbm, wmk_ref),
            (v_hbm, v_ref), (wfv_hbm, wfv_ref), (wmv_hbm, wmv_ref), (q_hbm, q_ref),
        ))
    ]
    for copy in fetches:
        copy.start()

    def loop(low, high, f):
        def step(i, _):
            f(i)
            return 0

        lax.fori_loop(low, high, step, 0)

    def at(linear):
        return (linear // cols, lax.rem(linear, cols))

    ahead = at(lax.rem(pos + 2, total))

    mid_buf[...] = jnp.zeros_like(mid_buf)

    def clear(c):
        far_buf[c] = jnp.zeros(far_buf.shape[1:], far_buf.dtype)

    loop(0, 2 * rows, clear)

    barrier = pltpu.get_barrier_semaphore()

    def greet(device):
        pl.semaphore_signal(barrier, inc=1, device_id=device, device_id_type=MESH)

    loop(1, cols, lambda i: greet((row, lax.rem(col + i, cols))))
    loop(0, pairs, lambda p: greet((other_row, 2 * p + side)))

    def greet_if(condition, device):
        @pl.when(condition)
        def _():
            greet(device)

        return condition.astype(jnp.int32)

    greeted = (
        cols - 1 + pairs
        + greet_if(jnp.logical_not(is_last), (row + 2, col))
        + greet_if(high > 0, (row - 2, col))
        + greet_if(pos + 2 < total, at(pos + 2))
        + greet_if(pos >= 2, at(pos - 2))
    )

    def head_lanes(h, base=0):
        return pl.ds(pl.multiple_of(base + h * DH, DH), DH)

    def remote(src, dst, send, recv, device):
        return pltpu.make_async_remote_copy(
            src_ref=src, dst_ref=dst, send_sem=send, recv_sem=recv,
            device_id=device, device_id_type=MESH,
        )

    def same(ref, send, recv, device):
        return remote(ref, ref, send, recv, device)

    def far_block(r, p):
        return far_buf.at[2 * r + side, pl.ds(pl.multiple_of(p * fars, fars), fars), :]

    def swap(p_to, p_from):
        return same(far_block(row, p_from), swap_send.at[p_to], swap_recv.at[p_from], (row, 2 * p_to + side))

    def side_swap(r, p_to, p_from):
        return same(far_block(r, p_from), side_send.at[p_to], side_recv.at[p_from], (other_row, 2 * p_to + side))

    def down(r):
        return same(far_buf.at[2 * r + side], down_send.at[r], down_recv.at[r], (row + 2, col))

    def cross(r):
        return same(far_buf.at[2 * r + side], cross_send.at[r], cross_recv.at[r], beside)

    def twin(r, s):
        return same(far_buf.at[2 * r + s], twin_send.at[r], twin_recv.at[r], partner)

    def mid_span(c):
        return mid_buf.at[pl.ds(pl.multiple_of(c * mids, mids), mids), :]

    def mid_copy(p_to, p_from):
        return same(mid_span(2 * p_from + side), mid_send.at[p_to], mid_recv.at[p_from], (row, 2 * p_to + side))

    def mid_pass(p, s):
        return same(mid_span(2 * p + s), pass_send.at[p], pass_recv.at[p], partner)

    def near_copy(i):
        return remote(
            own[i], near.at[FROM_PARTNER, i], near_send.at[FROM_PARTNER, i, 0],
            near_recv.at[FROM_PARTNER, i, 0], partner,
        )

    def behind_copy(i, h):
        lanes = head_lanes(h)
        return remote(
            own[i].at[:, lanes], near.at[FROM_BEHIND, i, :, lanes],
            near_send.at[FROM_BEHIND, i, h], near_recv.at[FROM_BEHIND, i, h], ahead,
        )

    def relay_copy(i, h):
        lanes = head_lanes(h)
        return remote(
            near.at[FROM_BEHIND, i, :, lanes], near.at[RELAYED, i, :, lanes],
            near_send.at[RELAYED, i, h], near_recv.at[RELAYED, i, h], partner,
        )

    def behind_start(h):
        for i in range(2):
            behind_copy(i, h).start()

    own = (k_ref, v_ref)
    mid_rows = pl.ds(pl.multiple_of(col * mids, mids), mids)
    far_rows = pl.ds(pl.multiple_of(pair * fars, fars), fars)

    def summarise(s, src, wm, wf):
        for copy in fetches[3 * s:3 * s + 3]:
            copy.wait()
        for h in range(HK):
            wide[s * HK + h] = src[:, h * DH:(h + 1) * DH].astype(jnp.float32)
        for squeeze, count, weight in ((FAR, fars, wf), (MID, mids, wm)):
            grouped = jnp.concatenate(
                [
                    jnp.concatenate(
                        [wide[s * HK + h, pl.ds(i, count, stride=squeeze), :] for h in range(HK)],
                        axis=0,
                    ).astype(jnp.bfloat16)
                    for i in range(squeeze)
                ],
                axis=1,
            )
            merged = jnp.dot(grouped, weight[...], preferred_element_type=jnp.float32)
            merged = merged.astype(jnp.bfloat16)
            for h in range(HK):
                lanes = slice(s * KV + h * DH, s * KV + (h + 1) * DH)
                piece = merged[h * count:(h + 1) * count]
                if squeeze == FAR:
                    far_buf[2 * row + side, far_rows, lanes] = piece
                else:
                    mid_buf[mid_rows, lanes] = piece

    def others(f):
        def one(p):
            @pl.when(p != pair)
            def _():
                f(p)

        loop(0, pairs, one)

    def when(condition, f):
        @pl.when(condition)
        def _():
            f()

    def side_pairs(f):
        loop(low, pairs, f)

    summarise(0, k_ref, wmk_ref, wfk_ref)
    summarise(1, v_ref, wmv_ref, wfv_ref)
    pl.semaphore_wait(barrier, greeted)

    others(lambda p: swap(p, pair).start())
    side_pairs(lambda p: side_swap(row, p, pair).start())
    loop(pair + 1, pairs, lambda p: mid_copy(p, pair).start())

    when(pos + 2 < total, lambda: behind_start(0))

    @pl.when(side == 0)
    def _():
        for i in range(2):
            near_copy(i).start()
        mid_pass(pair, 0).start()

    fetches[6].wait()

    def iota(shape, axis):
        return lax.broadcasted_iota(jnp.int32, shape, axis)

    def query(h, g):
        return q_ref[:, pl.ds(pl.multiple_of((h * GROUP + g) * DH, DH), DH)]

    def near_first(with_partner):
        def two(i):
            seen = iota((tok, tok), 0) <= iota((tok, tok), 1)
            work = []
            for h in (2 * i, 2 * i + 1):
                keys = [k_ref[:, head_lanes(h)]]
                flats = [flat(v_ref[:, head_lanes(h)])]
                if with_partner:
                    keys.append(near[FROM_PARTNER, 0, :, head_lanes(h)])
                    flats.append(flat(near[FROM_PARTNER, 1, :, head_lanes(h)]))
                for g in range(GROUP):
                    work.append((h * GROUP + g, [score(k, query(h, g)) for k in keys], flats))
            for n, parts, flats in work:
                parts = [jnp.where(seen, parts[0], NEG_FILL)] + parts[1:]
                top = top_of(parts)
                top_ref[n] = top
                den_ref[n], acc_ref[n] = weigh(parts, top, flats)

        return two

    def spread():
        others(lambda p: swap(p, p).wait_recv())

        @pl.when(jnp.logical_not(is_leaf))
        def _():
            loop(0, pairs, lambda p: side_swap(other_row, p, p).wait_recv())

            @pl.when(jnp.logical_not(is_last))
            def _():
                loop(0, 2, lambda i: down(2 * high + i).start())

        when(low == 1, lambda: twin(row - 1, side).start())
        when(pos + 2 < total, lambda: loop(1, HK, behind_start))

    def near_own(with_partner):
        two = near_first(with_partner)

        def step(i):
            two(i)
            when(i == 0, spread)

        loop(0, HK // 2, step)

    @pl.when(side == 0)
    def _():
        near_own(False)

    @pl.when(side == 1)
    def _():
        for i in range(2):
            near_copy(i).wait_recv()
        near_own(True)

    def mid_arrive(p):
        mid_copy(p, p).wait_recv()
        mid_pass(p, side).start()

    loop(0, pair, mid_arrive)
    loop(0, pair, lambda p: mid_pass(p, 1 - side).wait_recv())

    @pl.when(side == 1)
    def _():
        mid_pass(pair, 0).wait_recv()

    n_mid = mid_buf.shape[0]

    def mid_two(i):
        seen = (iota((n_mid, tok), 0) * MID + MID - 1) <= (iota((n_mid, tok), 1) + col * tok)
        work = []
        for h in (2 * i, 2 * i + 1):
            keys = mid_buf[:, head_lanes(h)]
            values = flat(mid_buf[:, head_lanes(h, KV)])
            for g in range(GROUP):
                work.append((h * GROUP + g, score(keys, query(h, g)), values))
        for n, s, values in work:
            s = jnp.where(seen, s, NEG_FILL)
            den, acc = weigh([s], jnp.maximum(top_of([s]), TOP_FLOOR), [values])
            rest_ref[n] = acc * inverse(den)

    loop(0, HK // 2, mid_two)

    def hand_on(k):
        def one(i):
            r = 2 * (high - 1 - k) + i

            @pl.when(is_leaf)
            def _():
                cross(r).wait_recv()

            @pl.when(jnp.logical_not(is_leaf))
            def _():
                down(r).wait_recv()
                when(jnp.logical_not(is_last), lambda: down(r).start())
                when((low == 1) & (pair == 0), lambda: cross(r).start())

            twin(r, side).start()

        loop(0, 2, one)

    def arrive(h):
        for i in range(2):
            behind_copy(i, h).wait_recv()
            relay_copy(i, h).start()

    def near_last(h):
        for i in range(2):
            relay_copy(i, h).wait_recv()
        slots = (FROM_BEHIND, RELAYED)
        keys = [near[slot, 0, :, head_lanes(h)] for slot in slots]
        flats = [flat(near[slot, 1, :, head_lanes(h)]) for slot in slots]
        work = [[score(k, query(h, g)) for k in keys] for g in range(GROUP)]
        for g, parts in enumerate(work):
            n = h * GROUP + g
            before = top_ref[n]
            top = jnp.maximum(before, top_of(parts))
            den, acc = weigh(parts, top, flats)
            fade = powers(before, top)
            den_ref[n] = den_ref[n] * fade + den
            acc_ref[n] = acc_ref[n] * fade + acc

    line = far_buf.shape[1]
    per = max(1, min(2 * rows, FAR_CHUNK // line))
    n_chunk = 2 * rows // per

    def far_two(i):
        def part(h, j, base):
            block = far_buf[pl.ds(j * per, per), :, head_lanes(h, base)]
            return block.reshape(per * line, DH)

        def chunk(j, carry):
            seen = iota((per * line, 1), 0) + j * (per * line) < 2 * row * line
            work = []
            for h in (2 * i, 2 * i + 1):
                keys, flats = part(h, j, 0), flat(part(h, j, KV))
                work += [(score(keys, query(h, g)), flats) for g in range(GROUP)]
            after = []
            for m, (s, flats) in enumerate(work):
                s = jnp.where(seen, s, NEG_FILL)
                top = top_of([s])
                if carry is None:
                    after.append((top, *weigh([s], top, [flats])))
                    continue
                before, den, acc = carry[m]
                top = jnp.maximum(before, top)
                fade = powers(before, top)
                more, extra = weigh([s], top, [flats])
                after.append((top, den * fade + more, acc * fade + extra))
            return after

        carry = chunk(0, None)
        if n_chunk > 1:
            carry = lax.fori_loop(1, (2 * row + per - 1) // per, chunk, carry)
        for m, (_, den, acc) in enumerate(carry):
            n = 2 * i * GROUP + m
            rest_ref[n] = rest_ref[n] + acc * inverse(den)

    def finish(h):
        for g in range(GROUP):
            n = h * GROUP + g
            whole = acc_ref[n] * inverse(den_ref[n]) + rest_ref[n]
            lanes = pl.ds(pl.multiple_of(n * DH, DH), DH)
            out_ref[:, lanes] = whole.astype(out_ref.dtype).T

    def near_step(h):
        when(h < high, lambda: hand_on(h))

        @pl.when(pos >= 2)
        def _():
            arrive(h)
            near_last(h)

    loop(0, HK - 1, near_step)

    loop(HK - 1, high, hand_on)

    loop(0, row, lambda r: twin(r, 1 - side).wait_recv())

    @pl.when(pos >= 2)
    def _():
        arrive(HK - 1)

    @pl.when(row > 0)
    def _():
        loop(0, HK // 2, far_two)

    loop(0, HK - 1, finish)

    @pl.when(pos >= 2)
    def _():
        near_last(HK - 1)

    finish(HK - 1)

    others(lambda p: swap(p, pair).wait_send())
    loop(pair + 1, pairs, lambda p: mid_copy(p, pair).wait_send())
    side_pairs(lambda p: side_swap(row, p, pair).wait_send())

    @pl.when(jnp.logical_not(is_leaf) & jnp.logical_not(is_last))
    def _():
        loop(0, 2 * high + 2, lambda r: down(r).wait_send())

    @pl.when((low == 1) & (pair == 0))
    def _():
        loop(0, 2 * high, lambda r: cross(r).wait_send())

    loop(0, pair, lambda p: mid_pass(p, side).wait_send())
    loop(0, row, lambda r: twin(r, side).wait_send())

    @pl.when(side == 0)
    def _():
        for i in range(2):
            near_copy(i).wait_send()
        mid_pass(pair, 0).wait_send()

    @pl.when(pos + 2 < total)
    def _():
        for i in range(2):
            loop(0, HK, lambda h, i=i: behind_copy(i, h).wait_send())

    @pl.when(pos >= 2)
    def _():
        for i in range(2):
            loop(0, HK, lambda h, i=i: relay_copy(i, h).wait_send())


def body(rows, cols, queries, keys, values, *weights):
    tok = queries.shape[0]
    assert BLOCK == 2 * tok and cols % 2 == 0 and rows % 2 == 0
    dma = pltpu.SemaphoreType.DMA
    bf16, f32 = jnp.bfloat16, jnp.float32
    vmem = pl.BlockSpec(memory_space=pltpu.VMEM)
    pairs = cols // 2
    return pl.pallas_call(
        functools.partial(kernel, rows, cols),
        out_shape=pltpu.VMEM(queries.shape, bf16),
        in_specs=[pl.BlockSpec(memory_space=pltpu.HBM)] * 7,
        out_specs=vmem,
        scratch_shapes=[
            *[pltpu.VMEM(a.shape, a.dtype) for a in (queries, keys, values, *weights)],
            dma((7,)),
            pltpu.VMEM((2 * HK, tok, DH), f32),
            pltpu.VMEM((cols * (tok // MID), 2 * KV), bf16),
            pltpu.VMEM((2 * rows, pairs * (tok // FAR), 2 * KV), bf16),
            pltpu.VMEM((3, 2, tok, KV), bf16),
            pltpu.VMEM((HQ, 1, tok), f32),
            pltpu.VMEM((HQ, 1, tok), f32),
            pltpu.VMEM((HQ, DH, tok), f32),
            pltpu.VMEM((HQ, DH, tok), f32),
            dma((3, 2, HK)),
            dma((3, 2, HK)),
            *[dma((pairs,))] * 8,
            *[dma((rows,))] * 6,
        ],
        compiler_params=pltpu.CompilerParams(
            collective_id=0, has_side_effects=True, vmem_limit_bytes=VMEM_LIMIT
        ),
    )(queries, keys, values, *weights)


def solution(mesh):
    spec = P(("row", "col"), None)
    return jax.shard_map(
        functools.partial(body, mesh.shape["row"], mesh.shape["col"]),
        mesh=mesh,
        in_specs=(spec, spec, spec, P(), P(), P(), P()),
        out_specs=spec,
        check_vma=False,
    )
```

time: 39.3 us -> 33.8 us (0.86)
  the two profiles are of different devices: /device:TPU:17 before, /device:TPU:31 now
where the time goes in v1:
time: 33.8 us; the launch traced here: 33.7 us
  Pallas kernels  32.7 us (97%)
  local copies, waits for them, and re-layouts  0.97 us (3%)
    pallas_call x1, Pallas kernels, body(): pl.pallas_call(functools.partial(kernel, rows, cols), out_shape=pltpu.VME...  32.7 us
    unnamed x1, local copies, waits for them, and re-layouts  0.97 us

profile of v1, /device:TPU:31, one launch (start us, length us, event | category | flops | bytes accessed | tf_op | source)
XLA Modules:
  0.0 33.7 jit_solution(15644182880399879506)
XLA Ops:
  0.0 32.7 %shard_map.73 = bf16[256,2048]{1,0:T(8,128)(2,1)S(1)} custom-call(bf16[256,2048]{1,0:T(8,128)(2,1)} %q_hbm.1, bf16[256,512]{1,0:T(8,128)(2,1)} %k_hbm.1, bf16[256,512]{1,0:T(8,128)(2,1)} %v_hbm.1, bf16[1024,128]{1,0:T(8,128)(2,1)} %wmk_hbm.1, bf16[1024,128]{1,0:T(8,128)(2,1)} %wmv_hbm.1, bf16[2048,128]{1,0:T(8,128)(2,1)} %wfk_hbm.1, bf16[2048,128]{1,0:T(8,128)(2,1)} %wfv_hbm.1), custom_call_target="tpu_custom_call" | custom-call | tf_op jit(solution)/shard_map/pallas_call | solution.py:503
  32.7 1.0 %copy.9 = bf16[256,2048]{1,0:T(8,128)(2,1)} copy(bf16[256,2048]{1,0:T(8,128)(2,1)S(1)} %shard_map.73) | data formatting | bytes 2097152

commit v2 on v1

--- a/solution.py
+++ b/solution.py
@@ -20,7 +20,7 @@
 TOP_FLOOR = -1e29
 SUM_ROWS = 16
 EXP_SCALE = DH ** (-0.5) * math.log2(math.e)
-FAR_CHUNK = 512
+FAR_CHUNK = 256
 VMEM_LIMIT = 57 * 1024 * 1024
 MESH = pl.DeviceIdType.MESH
 FROM_PARTNER, FROM_BEHIND, RELAYED = 0, 1, 2
@@ -60,9 +60,10 @@
     q_hbm, k_hbm, v_hbm, wmk_hbm, wmv_hbm, wfk_hbm, wfv_hbm, out_ref,
     q_ref, k_ref, v_ref, wmk_ref, wmv_ref, wfk_ref, wfv_ref, fetch_sem,
     wide, mid_buf, far_buf, near, top_ref, den_ref, acc_ref, rest_ref,
+    far_top, far_den, far_acc,
     near_send, near_recv, mid_send, mid_recv, pass_send, pass_recv,
     swap_send, swap_recv, side_send, side_recv,
-    down_send, down_recv, cross_send, cross_recv, twin_send, twin_recv,
+    down_send, down_recv, cross_send, cross_recv, lift_send, lift_recv, twin_send, twin_recv,
 ):
     tok = q_ref.shape[0]
     mids, fars = tok // MID, tok // FAR
@@ -77,7 +78,9 @@
     other_row = row + 1 - 2 * low
     partner = (row, col + 1 - 2 * side)
     beside = (other_row, col)
-    is_leaf = (low == 0) & (pair == 0)
+    is_hub = (low == 1) & (pair == pairs - 1)
+    feeds_beside = (low == 0) & (pair == pairs - 1)
+    feeds_next = (low == 1) & (pair == pairs - 2)
     is_last = high + 1 == rows // 2
 
     def fetch(i, src, dst):
@@ -86,8 +89,8 @@
     fetches = [
         fetch(i, src, dst)
         for i, (src, dst) in enumerate((
-            (k_hbm, k_ref), (wfk_hbm, wfk_ref), (wmk_hbm, wmk_ref),
-            (v_hbm, v_ref), (wfv_hbm, wfv_ref), (wmv_hbm, wmv_ref), (q_hbm, q_ref),
+            (k_hbm, k_ref), (v_hbm, v_ref), (wfk_hbm, wfk_ref), (wfv_hbm, wfv_ref),
+            (wmk_hbm, wmk_ref), (wmv_hbm, wmv_ref), (q_hbm, q_ref),
         ))
     ]
     for copy in fetches:
@@ -106,6 +109,14 @@
     ahead = at(lax.rem(pos + 2, total))
 
     mid_buf[...] = jnp.zeros_like(mid_buf)
+
+    far_top[...] = jnp.full_like(far_top, TOP_FLOOR)
+    far_den[...] = jnp.zeros_like(far_den)
+
+    def reset(n):
+        far_acc[n] = jnp.zeros(far_acc.shape[1:], far_acc.dtype)
+
+    loop(0, HQ, reset)
 
     def clear(c):
         far_buf[c] = jnp.zeros(far_buf.shape[1:], far_buf.dtype)
@@ -162,6 +173,9 @@
     def cross(r):
         return same(far_buf.at[2 * r + side], cross_send.at[r], cross_recv.at[r], beside)
 
+    def lift(r):
+        return same(far_buf.at[2 * r + side], lift_send.at[r], lift_recv.at[r], (row, col + 2))
+
     def twin(r, s):
         return same(far_buf.at[2 * r + s], twin_send.at[r], twin_recv.at[r], partner)
 
@@ -174,11 +188,17 @@
     def mid_pass(p, s):
         return same(mid_span(2 * p + s), pass_send.at[p], pass_recv.at[p], partner)
 
-    def near_copy(i):
+    def near_copy(i, half):
+        lanes = pl.ds(pl.multiple_of(half * (KV // 2), KV // 2), KV // 2)
         return remote(
-            own[i], near.at[FROM_PARTNER, i], near_send.at[FROM_PARTNER, i, 0],
-            near_recv.at[FROM_PARTNER, i, 0], partner,
+            own[i].at[:, lanes], near.at[FROM_PARTNER, i, :, lanes],
+            near_send.at[FROM_PARTNER, i, half], near_recv.at[FROM_PARTNER, i, half], partner,
         )
+
+    def halves(f):
+        for half in range(2):
+            for i in range(2):
+                f(near_copy(i, half))
 
     def behind_copy(i, h):
         lanes = head_lanes(h)
@@ -202,31 +222,31 @@
     mid_rows = pl.ds(pl.multiple_of(col * mids, mids), mids)
     far_rows = pl.ds(pl.multiple_of(pair * fars, fars), fars)
 
-    def summarise(s, src, wm, wf):
-        for copy in fetches[3 * s:3 * s + 3]:
-            copy.wait()
+    def spread_out(s, src):
         for h in range(HK):
             wide[s * HK + h] = src[:, h * DH:(h + 1) * DH].astype(jnp.float32)
-        for squeeze, count, weight in ((FAR, fars, wf), (MID, mids, wm)):
-            grouped = jnp.concatenate(
-                [
-                    jnp.concatenate(
-                        [wide[s * HK + h, pl.ds(i, count, stride=squeeze), :] for h in range(HK)],
-                        axis=0,
-                    ).astype(jnp.bfloat16)
-                    for i in range(squeeze)
-                ],
-                axis=1,
-            )
-            merged = jnp.dot(grouped, weight[...], preferred_element_type=jnp.float32)
-            merged = merged.astype(jnp.bfloat16)
-            for h in range(HK):
-                lanes = slice(s * KV + h * DH, s * KV + (h + 1) * DH)
-                piece = merged[h * count:(h + 1) * count]
-                if squeeze == FAR:
-                    far_buf[2 * row + side, far_rows, lanes] = piece
-                else:
-                    mid_buf[mid_rows, lanes] = piece
+
+    def summarise(s, squeeze, weight):
+        count = tok // squeeze
+        grouped = jnp.concatenate(
+            [
+                jnp.concatenate(
+                    [wide[s * HK + h, pl.ds(i, count, stride=squeeze), :] for h in range(HK)],
+                    axis=0,
+                ).astype(jnp.bfloat16)
+                for i in range(squeeze)
+            ],
+            axis=1,
+        )
+        merged = jnp.dot(grouped, weight[...], preferred_element_type=jnp.float32)
+        merged = merged.astype(jnp.bfloat16)
+        for h in range(HK):
+            lanes = slice(s * KV + h * DH, s * KV + (h + 1) * DH)
+            piece = merged[h * count:(h + 1) * count]
+            if squeeze == FAR:
+                far_buf[2 * row + side, far_rows, lanes] = piece
+            else:
+                mid_buf[mid_rows, lanes] = piece
 
     def others(f):
         def one(p):
@@ -241,24 +261,28 @@
         def _():
             f()
 
-    def side_pairs(f):
-        loop(low, pairs, f)
-
-    summarise(0, k_ref, wmk_ref, wfk_ref)
-    summarise(1, v_ref, wmv_ref, wfv_ref)
+    for copy in fetches[:2]:
+        copy.wait()
     pl.semaphore_wait(barrier, greeted)
-
+    when(side == 0, lambda: halves(lambda copy: copy.start()))
+    spread_out(0, k_ref)
+    spread_out(1, v_ref)
+    for copy in fetches[2:4]:
+        copy.wait()
+    summarise(0, FAR, wfk_ref)
+    summarise(1, FAR, wfv_ref)
     others(lambda p: swap(p, pair).start())
-    side_pairs(lambda p: side_swap(row, p, pair).start())
+    loop(0, pairs, lambda p: side_swap(row, p, pair).start())
+    for copy in fetches[4:6]:
+        copy.wait()
+    summarise(0, MID, wmk_ref)
+    summarise(1, MID, wmv_ref)
     loop(pair + 1, pairs, lambda p: mid_copy(p, pair).start())
-
-    when(pos + 2 < total, lambda: behind_start(0))
-
-    @pl.when(side == 0)
-    def _():
-        for i in range(2):
-            near_copy(i).start()
-        mid_pass(pair, 0).start()
+    when(side == 0, lambda: mid_pass(pair, 0).start())
+
+    leads = pair == pairs - 1
+    sends = pos + 2 < total
+    when(feeds_beside & sends, lambda: behind_start(0))
 
     fetches[6].wait()
 
@@ -272,6 +296,9 @@
         def two(i):
             seen = iota((tok, tok), 0) <= iota((tok, tok), 1)
             work = []
+            if with_partner:
+                near_copy(0, i).wait_recv()
+                near_copy(1, i).wait_recv()
             for h in (2 * i, 2 * i + 1):
                 keys = [k_ref[:, head_lanes(h)]]
                 flats = [flat(v_ref[:, head_lanes(h)])]
@@ -290,24 +317,27 @@
 
     def spread():
         others(lambda p: swap(p, p).wait_recv())
-
-        @pl.when(jnp.logical_not(is_leaf))
-        def _():
-            loop(0, pairs, lambda p: side_swap(other_row, p, p).wait_recv())
-
-            @pl.when(jnp.logical_not(is_last))
-            def _():
-                loop(0, 2, lambda i: down(2 * high + i).start())
-
+        others(lambda p: side_swap(other_row, p, p).wait_recv())
+        when(jnp.logical_not(is_last), lambda: loop(0, 2, lambda i: down(2 * high + i).start()))
+        when(leads & sends, lambda: loop(2, HK, behind_start))
         when(low == 1, lambda: twin(row - 1, side).start())
-        when(pos + 2 < total, lambda: loop(1, HK, behind_start))
+
+    def near_more():
+        side_swap(other_row, pair, pair).wait_recv()
+        when(sends, lambda: loop(jnp.where(feeds_beside, 1, 0), jnp.where(leads, 2, HK), behind_start))
 
     def near_own(with_partner):
         two = near_first(with_partner)
 
         def step(i):
+            if with_partner:
+                when(i == 0, near_more)
             two(i)
-            when(i == 0, spread)
+            if with_partner:
+                when(i == 0, spread)
+            else:
+                when(i == 0, near_more)
+                when(i == 1, spread)
 
         loop(0, HK // 2, step)
 
@@ -317,8 +347,6 @@
 
     @pl.when(side == 1)
     def _():
-        for i in range(2):
-            near_copy(i).wait_recv()
         near_own(True)
 
     def mid_arrive(p):
@@ -353,15 +381,18 @@
         def one(i):
             r = 2 * (high - 1 - k) + i
 
-            @pl.when(is_leaf)
+            @pl.when(is_hub)
             def _():
-                cross(r).wait_recv()
-
-            @pl.when(jnp.logical_not(is_leaf))
+                when(k == 0, lambda: down(r).wait_recv())
+                when(k == 1, lambda: cross(r).wait_recv())
+                when(k > 1, lambda: lift(r).wait_recv())
+
+            @pl.when(jnp.logical_not(is_hub))
             def _():
                 down(r).wait_recv()
                 when(jnp.logical_not(is_last), lambda: down(r).start())
-                when((low == 1) & (pair == 0), lambda: cross(r).start())
+                when(feeds_beside & (k == 1), lambda: cross(r).start())
+                when(feeds_next & (k > 1), lambda: lift(r).start())
 
             twin(r, side).start()
 
@@ -390,96 +421,104 @@
 
     line = far_buf.shape[1]
     per = max(1, min(2 * rows, FAR_CHUNK // line))
-    n_chunk = 2 * rows // per
-
-    def far_two(i):
-        def part(h, j, base):
+    def far_two(j, i):
+        def part(h, base):
             block = far_buf[pl.ds(j * per, per), :, head_lanes(h, base)]
             return block.reshape(per * line, DH)
 
-        def chunk(j, carry):
-            seen = iota((per * line, 1), 0) + j * (per * line) < 2 * row * line
-            work = []
-            for h in (2 * i, 2 * i + 1):
-                keys, flats = part(h, j, 0), flat(part(h, j, KV))
-                work += [(score(keys, query(h, g)), flats) for g in range(GROUP)]
-            after = []
-            for m, (s, flats) in enumerate(work):
-                s = jnp.where(seen, s, NEG_FILL)
-                top = top_of([s])
-                if carry is None:
-                    after.append((top, *weigh([s], top, [flats])))
-                    continue
-                before, den, acc = carry[m]
-                top = jnp.maximum(before, top)
-                fade = powers(before, top)
-                more, extra = weigh([s], top, [flats])
-                after.append((top, den * fade + more, acc * fade + extra))
-            return after
-
-        carry = chunk(0, None)
-        if n_chunk > 1:
-            carry = lax.fori_loop(1, (2 * row + per - 1) // per, chunk, carry)
-        for m, (_, den, acc) in enumerate(carry):
-            n = 2 * i * GROUP + m
-            rest_ref[n] = rest_ref[n] + acc * inverse(den)
-
-    def finish(h):
+        seen = iota((per * line, 1), 0) + j * (per * line) < 2 * row * line
+        work = []
+        for h in (2 * i, 2 * i + 1):
+            keys, flats = part(h, 0), flat(part(h, KV))
+            work += [(h * GROUP + g, score(keys, query(h, g)), flats) for g in range(GROUP)]
+        for n, s, flats in work:
+            s = jnp.where(seen, s, NEG_FILL)
+            before = far_top[n]
+            top = jnp.maximum(before, top_of([s]))
+            fade = powers(before, top)
+            den, acc = weigh([s], top, [flats])
+            far_top[n] = top
+            far_den[n] = far_den[n] * fade + den
+            far_acc[n] = far_acc[n] * fade + acc
+
+    row_span = per // 2
+    newest = (row + row_span - 1) // row_span - 1
+
+    def far_chunks(name, low_chunk, high_chunk):
+        loop(low_chunk * row_span, jnp.minimum(high_chunk * row_span, row), lambda r: twin(r, 1 - side).wait_recv())
+        loop(low_chunk, high_chunk, lambda j: loop(0, HK // 2, functools.partial(far_two, j)))
+
+    early = jnp.logical_not(is_hub) | (newest * row_span >= 2 * high)
+
+    def finish(with_far, h):
         for g in range(GROUP):
             n = h * GROUP + g
             whole = acc_ref[n] * inverse(den_ref[n]) + rest_ref[n]
+            if with_far:
+                whole = whole + far_acc[n] * inverse(far_den[n])
             lanes = pl.ds(pl.multiple_of(n * DH, DH), DH)
             out_ref[:, lanes] = whole.astype(out_ref.dtype).T
 
+    def near_in(h):
+        when(pos >= 2, lambda: arrive(h))
+
     def near_step(h):
-        when(h < high, lambda: hand_on(h))
+        when((h < high) & jnp.logical_not(is_hub), lambda: hand_on(h))
+        near_in(h)
+        when((h == 1) & (row > 0) & early, lambda: far_chunks("FAR1", newest, newest + 1))
 
         @pl.when(pos >= 2)
         def _():
-            arrive(h)
             near_last(h)
 
     loop(0, HK - 1, near_step)
 
-    loop(HK - 1, high, hand_on)
-
-    loop(0, row, lambda r: twin(r, 1 - side).wait_recv())
-
-    @pl.when(pos >= 2)
-    def _():
-        arrive(HK - 1)
+    @pl.when(is_hub & (high > 0))
+    def _():
+        hand_on(0)
+        when(jnp.logical_not(early), lambda: far_chunks("FAR3", newest, newest + 1))
+
+    loop(jnp.where(is_hub, 1, HK - 1), high, hand_on)
+    near_in(HK - 1)
 
     @pl.when(row > 0)
     def _():
-        loop(0, HK // 2, far_two)
-
-    loop(0, HK - 1, finish)
-
-    @pl.when(pos >= 2)
-    def _():
+        far_chunks("FAR2", 0, newest)
+        loop(0, HK - 1, functools.partial(finish, True))
         near_last(HK - 1)
-
-    finish(HK - 1)
+        finish(True, HK - 1)
+
+    @pl.when(row == 0)
+    def _():
+        @pl.when(pos >= 2)
+        def _():
+            near_last(HK - 1)
+
+        loop(0, HK, functools.partial(finish, False))
 
     others(lambda p: swap(p, pair).wait_send())
     loop(pair + 1, pairs, lambda p: mid_copy(p, pair).wait_send())
-    side_pairs(lambda p: side_swap(row, p, pair).wait_send())
-
-    @pl.when(jnp.logical_not(is_leaf) & jnp.logical_not(is_last))
-    def _():
-        loop(0, 2 * high + 2, lambda r: down(r).wait_send())
-
-    @pl.when((low == 1) & (pair == 0))
-    def _():
-        loop(0, 2 * high, lambda r: cross(r).wait_send())
+    loop(0, pairs, lambda p: side_swap(row, p, pair).wait_send())
 
     loop(0, pair, lambda p: mid_pass(p, side).wait_send())
+
+    @pl.when(jnp.logical_not(is_last))
+    def _():
+        loop(jnp.where(is_hub, 2 * high, 0), 2 * high + 2, lambda r: down(r).wait_send())
+
+    @pl.when(feeds_beside & (high > 1))
+    def _():
+        loop(2 * high - 4, 2 * high - 2, lambda r: cross(r).wait_send())
+
+    @pl.when(feeds_next)
+    def _():
+        loop(0, 2 * high - 4, lambda r: lift(r).wait_send())
+
     loop(0, row, lambda r: twin(r, side).wait_send())
 
     @pl.when(side == 0)
     def _():
-        for i in range(2):
-            near_copy(i).wait_send()
+        halves(lambda copy: copy.wait_send())
         mid_pass(pair, 0).wait_send()
 
     @pl.when(pos + 2 < total)
@@ -516,10 +555,13 @@
             pltpu.VMEM((HQ, 1, tok), f32),
             pltpu.VMEM((HQ, DH, tok), f32),
             pltpu.VMEM((HQ, DH, tok), f32),
+            pltpu.VMEM((HQ, 1, tok), f32),
+            pltpu.VMEM((HQ, 1, tok), f32),
+            pltpu.VMEM((HQ, DH, tok), f32),
             dma((3, 2, HK)),
             dma((3, 2, HK)),
             *[dma((pairs,))] * 8,
-            *[dma((rows,))] * 6,
+            *[dma((rows,))] * 8,
         ],
         compiler_params=pltpu.CompilerParams(
             collective_id=0, has_side_effects=True, vmem_limit_bytes=VMEM_LIMIT

time: 33.8 us -> 29.6 us (0.88)
  Pallas kernels: 32.7 us -> 28.5 us
    pallas_call x1, Pallas kernels: 32.7 us -> 28.5 us  [body(): pl.pallas_call(functools.partial(kernel, rows, cols), out_shape=pltpu.VME...]
where the time goes in v2:
time: 29.6 us; the launch traced here: 29.5 us
  Pallas kernels  28.5 us (96%)
  local copies, waits for them, and re-layouts  0.97 us (3%)
    pallas_call x1, Pallas kernels, body(): pl.pallas_call(functools.partial(kernel, rows, cols), out_shape=pltpu.VME...  28.5 us
    unnamed x1, local copies, waits for them, and re-layouts  0.97 us

profile of v2, /device:TPU:31, one launch (start us, length us, event | category | flops | bytes accessed | tf_op | source)
XLA Modules:
  0.0 29.5 jit_solution(16086538902035954726)
XLA Ops:
  0.0 28.5 %shard_map.73 = bf16[256,2048]{1,0:T(8,128)(2,1)S(1)} custom-call(bf16[256,2048]{1,0:T(8,128)(2,1)} %q_hbm.1, bf16[256,512]{1,0:T(8,128)(2,1)} %k_hbm.1, bf16[256,512]{1,0:T(8,128)(2,1)} %v_hbm.1, bf16[1024,128]{1,0:T(8,128)(2,1)} %wmk_hbm.1, bf16[1024,128]{1,0:T(8,128)(2,1)} %wmv_hbm.1, bf16[2048,128]{1,0:T(8,128)(2,1)} %wfk_hbm.1, bf16[2048,128]{1,0:T(8,128)(2,1)} %wfv_hbm.1), custom_call_target="tpu_custom_call" | custom-call | tf_op jit(solution)/shard_map/pallas_call | solution.py:542
  28.5 1.0 %copy.9 = bf16[256,2048]{1,0:T(8,128)(2,1)} copy(bf16[256,2048]{1,0:T(8,128)(2,1)S(1)} %shard_map.73) | data formatting | bytes 2097152

commit v3 on v2

--- a/solution.py
+++ b/solution.py
@@ -19,6 +19,7 @@
 NEG_FILL = -1e30
 TOP_FLOOR = -1e29
 SUM_ROWS = 16
+N_FIRST = 2
 EXP_SCALE = DH ** (-0.5) * math.log2(math.e)
 FAR_CHUNK = 256
 VMEM_LIMIT = 57 * 1024 * 1024
@@ -62,7 +63,7 @@
     wide, mid_buf, far_buf, near, top_ref, den_ref, acc_ref, rest_ref,
     far_top, far_den, far_acc,
     near_send, near_recv, mid_send, mid_recv, pass_send, pass_recv,
-    swap_send, swap_recv, side_send, side_recv,
+    swap_send, swap_recv, side_send, side_recv, up_send,
     down_send, down_recv, cross_send, cross_recv, lift_send, lift_recv, twin_send, twin_recv,
 ):
     tok = q_ref.shape[0]
@@ -129,7 +130,7 @@
         pl.semaphore_signal(barrier, inc=1, device_id=device, device_id_type=MESH)
 
     loop(1, cols, lambda i: greet((row, lax.rem(col + i, cols))))
-    loop(0, pairs, lambda p: greet((other_row, 2 * p + side)))
+    greet((other_row, col))
 
     def greet_if(condition, device):
         @pl.when(condition)
@@ -139,7 +140,7 @@
         return condition.astype(jnp.int32)
 
     greeted = (
-        cols - 1 + pairs
+        cols
         + greet_if(jnp.logical_not(is_last), (row + 2, col))
         + greet_if(high > 0, (row - 2, col))
         + greet_if(pos + 2 < total, at(pos + 2))
@@ -164,8 +165,11 @@
     def swap(p_to, p_from):
         return same(far_block(row, p_from), swap_send.at[p_to], swap_recv.at[p_from], (row, 2 * p_to + side))
 
-    def side_swap(r, p_to, p_from):
-        return same(far_block(r, p_from), side_send.at[p_to], side_recv.at[p_from], (other_row, 2 * p_to + side))
+    def side_swap(r, p):
+        return same(far_block(r, p), side_send.at[p], side_recv.at[p], beside)
+
+    def up(p):
+        return same(far_block(other_row, pair), up_send.at[p], side_recv.at[pair], (row, 2 * p + side))
 
     def down(r):
         return same(far_buf.at[2 * r + side], down_send.at[r], down_recv.at[r], (row + 2, col))
@@ -263,16 +267,16 @@
 
     for copy in fetches[:2]:
         copy.wait()
-    pl.semaphore_wait(barrier, greeted)
-    when(side == 0, lambda: halves(lambda copy: copy.start()))
     spread_out(0, k_ref)
     spread_out(1, v_ref)
     for copy in fetches[2:4]:
         copy.wait()
     summarise(0, FAR, wfk_ref)
     summarise(1, FAR, wfv_ref)
+    pl.semaphore_wait(barrier, greeted)
     others(lambda p: swap(p, pair).start())
-    loop(0, pairs, lambda p: side_swap(row, p, pair).start())
+    side_swap(row, pair).start()
+    when(side == 0, lambda: halves(lambda copy: copy.start()))
     for copy in fetches[4:6]:
         copy.wait()
     summarise(0, MID, wmk_ref)
@@ -280,9 +284,8 @@
     loop(pair + 1, pairs, lambda p: mid_copy(p, pair).start())
     when(side == 0, lambda: mid_pass(pair, 0).start())
 
-    leads = pair == pairs - 1
     sends = pos + 2 < total
-    when(feeds_beside & sends, lambda: behind_start(0))
+    n_first = jnp.where(is_hub, N_FIRST, HK)
 
     fetches[6].wait()
 
@@ -316,15 +319,23 @@
         return two
 
     def spread():
-        others(lambda p: swap(p, p).wait_recv())
-        others(lambda p: side_swap(other_row, p, p).wait_recv())
-        when(jnp.logical_not(is_last), lambda: loop(0, 2, lambda i: down(2 * high + i).start()))
-        when(leads & sends, lambda: loop(2, HK, behind_start))
+        others(lambda p: side_swap(other_row, p).wait_recv())
+        when(jnp.logical_not(is_last), lambda: down(other_row).start())
+        when(sends, lambda: loop(n_first, HK, behind_start))
         when(low == 1, lambda: twin(row - 1, side).start())
 
     def near_more():
-        side_swap(other_row, pair, pair).wait_recv()
-        when(sends, lambda: loop(jnp.where(feeds_beside, 1, 0), jnp.where(leads, 2, HK), behind_start))
+        side_swap(other_row, pair).wait_recv()
+        loop(pair + 1, pairs, lambda p: up(p).start())
+
+        def over(p):
+            swap(p, p).wait_recv()
+            side_swap(row, p).start()
+
+        loop(pair + 1, pairs, over)
+        loop(0, pair, lambda p: swap(p, p).wait_recv())
+        when(sends, lambda: loop(0, n_first, behind_start))
+        when(jnp.logical_not(is_last), lambda: down(row).start())
 
     def near_own(with_partner):
         two = near_first(with_partner)
@@ -362,10 +373,10 @@
 
     n_mid = mid_buf.shape[0]
 
-    def mid_two(i):
+    def mid_all():
         seen = (iota((n_mid, tok), 0) * MID + MID - 1) <= (iota((n_mid, tok), 1) + col * tok)
         work = []
-        for h in (2 * i, 2 * i + 1):
+        for h in range(HK):
             keys = mid_buf[:, head_lanes(h)]
             values = flat(mid_buf[:, head_lanes(h, KV)])
             for g in range(GROUP):
@@ -375,11 +386,11 @@
             den, acc = weigh([s], jnp.maximum(top_of([s]), TOP_FLOOR), [values])
             rest_ref[n] = acc * inverse(den)
 
-    loop(0, HK // 2, mid_two)
+    mid_all()
 
     def hand_on(k):
         def one(i):
-            r = 2 * (high - 1 - k) + i
+            r = 2 * (high - 1 - k) + lax.rem(low + i, 2)
 
             @pl.when(is_hub)
             def _():
@@ -421,14 +432,14 @@
 
     line = far_buf.shape[1]
     per = max(1, min(2 * rows, FAR_CHUNK // line))
-    def far_two(j, i):
+    def far_chunk(j):
         def part(h, base):
             block = far_buf[pl.ds(j * per, per), :, head_lanes(h, base)]
             return block.reshape(per * line, DH)
 
         seen = iota((per * line, 1), 0) + j * (per * line) < 2 * row * line
         work = []
-        for h in (2 * i, 2 * i + 1):
+        for h in range(HK):
             keys, flats = part(h, 0), flat(part(h, KV))
             work += [(h * GROUP + g, score(keys, query(h, g)), flats) for g in range(GROUP)]
         for n, s, flats in work:
@@ -446,9 +457,7 @@
 
     def far_chunks(name, low_chunk, high_chunk):
         loop(low_chunk * row_span, jnp.minimum(high_chunk * row_span, row), lambda r: twin(r, 1 - side).wait_recv())
-        loop(low_chunk, high_chunk, lambda j: loop(0, HK // 2, functools.partial(far_two, j)))
-
-    early = jnp.logical_not(is_hub) | (newest * row_span >= 2 * high)
+        loop(low_chunk, high_chunk, far_chunk)
 
     def finish(with_far, h):
         for g in range(GROUP):
@@ -459,67 +468,84 @@
             lanes = pl.ds(pl.multiple_of(n * DH, DH), DH)
             out_ref[:, lanes] = whole.astype(out_ref.dtype).T
 
+    def sent_early():
+        others(lambda p: swap(p, pair).wait_send())
+        loop(pair + 1, pairs, lambda p: mid_copy(p, pair).wait_send())
+        loop(pair, pairs, lambda p: side_swap(row, p).wait_send())
+        loop(pair + 1, pairs, lambda p: up(p).wait_send())
+        loop(0, pair, lambda p: mid_pass(p, side).wait_send())
+
+        @pl.when(side == 0)
+        def _():
+            halves(lambda copy: copy.wait_send())
+            mid_pass(pair, 0).wait_send()
+
+    def feeds_next_done():
+        @pl.when(jnp.logical_not(is_last))
+        def _():
+            loop(jnp.where(is_hub, 2 * high, 0), 2 * high + 2, lambda r: down(r).wait_send())
+
+        @pl.when(feeds_beside & (high > 1))
+        def _():
+            loop(2 * high - 4, 2 * high - 2, lambda r: cross(r).wait_send())
+
+        @pl.when(feeds_next)
+        def _():
+            loop(0, 2 * high - 4, lambda r: lift(r).wait_send())
+
     def near_in(h):
         when(pos >= 2, lambda: arrive(h))
 
-    def near_step(h):
-        when((h < high) & jnp.logical_not(is_hub), lambda: hand_on(h))
-        near_in(h)
-        when((h == 1) & (row > 0) & early, lambda: far_chunks("FAR1", newest, newest + 1))
-
+    def near_end(h):
         @pl.when(pos >= 2)
         def _():
             near_last(h)
 
-    loop(0, HK - 1, near_step)
-
-    @pl.when(is_hub & (high > 0))
-    def _():
-        hand_on(0)
-        when(jnp.logical_not(early), lambda: far_chunks("FAR3", newest, newest + 1))
-
-    loop(jnp.where(is_hub, 1, HK - 1), high, hand_on)
-    near_in(HK - 1)
+    def far_newest():
+        far_chunks("FAR1", newest, newest + 1)
+
+    def far_rest():
+        far_chunks("FAR2", 0, newest)
+
+    plain = jnp.logical_not(is_hub)
+    far_first = (low == 0) & (pair == 0)
+
+    def step(s):
+        when((s == 0) & (high > 0) & plain, lambda: hand_on(0))
+        when((s < HK) & (s != 2), lambda: near_in(s))
+        when((s == 1) & plain & (high > 1), lambda: hand_on(1))
+        when(s > 0, lambda: near_end(s - 1))
+
+        @pl.when(s == 2)
+        def _():
+            loop(jnp.where(is_hub, 0, 2), jnp.where(is_hub, jnp.minimum(high, 1), high), hand_on)
+
+            def far(i):
+                when((i == 0) != far_first, lambda: near_in(2))
+                when((row > 0) & (i == 0), far_newest)
+
+            loop(0, 2, far)
+            when((row > 0) & plain, far_rest)
+
+        @pl.when(s == HK - 1)
+        def _():
+            sent_early()
+            when(is_hub, lambda: loop(1, high, hand_on))
+            when(plain & (row > 0), lambda: loop(0, HK - 1, functools.partial(finish, True)))
+
+    loop(0, HK + 1, step)
 
     @pl.when(row > 0)
     def _():
-        far_chunks("FAR2", 0, newest)
-        loop(0, HK - 1, functools.partial(finish, True))
-        near_last(HK - 1)
-        finish(True, HK - 1)
+        when(is_hub, far_rest)
+        loop(jnp.where(is_hub, 0, HK - 1), HK, functools.partial(finish, True))
 
     @pl.when(row == 0)
     def _():
-        @pl.when(pos >= 2)
-        def _():
-            near_last(HK - 1)
-
         loop(0, HK, functools.partial(finish, False))
 
-    others(lambda p: swap(p, pair).wait_send())
-    loop(pair + 1, pairs, lambda p: mid_copy(p, pair).wait_send())
-    loop(0, pairs, lambda p: side_swap(row, p, pair).wait_send())
-
-    loop(0, pair, lambda p: mid_pass(p, side).wait_send())
-
-    @pl.when(jnp.logical_not(is_last))
-    def _():
-        loop(jnp.where(is_hub, 2 * high, 0), 2 * high + 2, lambda r: down(r).wait_send())
-
-    @pl.when(feeds_beside & (high > 1))
-    def _():
-        loop(2 * high - 4, 2 * high - 2, lambda r: cross(r).wait_send())
-
-    @pl.when(feeds_next)
-    def _():
-        loop(0, 2 * high - 4, lambda r: lift(r).wait_send())
-
     loop(0, row, lambda r: twin(r, side).wait_send())
-
-    @pl.when(side == 0)
-    def _():
-        halves(lambda copy: copy.wait_send())
-        mid_pass(pair, 0).wait_send()
+    feeds_next_done()
 
     @pl.when(pos + 2 < total)
     def _():
@@ -560,7 +586,7 @@
             pltpu.VMEM((HQ, DH, tok), f32),
             dma((3, 2, HK)),
             dma((3, 2, HK)),
-            *[dma((pairs,))] * 8,
+            *[dma((pairs,))] * 9,
             *[dma((rows,))] * 8,
         ],
         compiler_params=pltpu.CompilerParams(

time: 29.6 us -> 26.7 us (0.902)
  Pallas kernels: 28.5 us -> 25.5 us
    pallas_call x1, Pallas kernels: 28.5 us -> 25.5 us  [body(): pl.pallas_call(functools.partial(kernel, rows, cols), out_shape=pltpu.VME...]
where the time goes in v3:
time: 26.7 us; the launch traced here: 26.5 us
  Pallas kernels  25.5 us (96%)
  local copies, waits for them, and re-layouts  0.97 us (4%)
    pallas_call x1, Pallas kernels, body(): pl.pallas_call(functools.partial(kernel, rows, cols), out_shape=pltpu.VME...  25.5 us
    unnamed x1, local copies, waits for them, and re-layouts  0.97 us

profile of v3, /device:TPU:31, one launch (start us, length us, event | category | flops | bytes accessed | tf_op | source)
XLA Modules:
  0.0 26.5 jit_solution(9192952082792812324)
XLA Ops:
  0.0 25.5 %shard_map.73 = bf16[256,2048]{1,0:T(8,128)(2,1)S(1)} custom-call(bf16[256,2048]{1,0:T(8,128)(2,1)} %q_hbm.1, bf16[256,512]{1,0:T(8,128)(2,1)} %k_hbm.1, bf16[256,512]{1,0:T(8,128)(2,1)} %v_hbm.1, bf16[1024,128]{1,0:T(8,128)(2,1)} %wmk_hbm.1, bf16[1024,128]{1,0:T(8,128)(2,1)} %wmv_hbm.1, bf16[2048,128]{1,0:T(8,128)(2,1)} %wfk_hbm.1, bf16[2048,128]{1,0:T(8,128)(2,1)} %wfv_hbm.1), custom_call_target="tpu_custom_call" | custom-call | tf_op jit(solution)/shard_map/pallas_call | solution.py:568
  25.6 1.0 %copy.9 = bf16[256,2048]{1,0:T(8,128)(2,1)} copy(bf16[256,2048]{1,0:T(8,128)(2,1)S(1)} %shard_map.73) | data formatting | bytes 2097152

commit v4 on v3

--- a/solution.py
+++ b/solution.py
@@ -21,7 +21,7 @@
 SUM_ROWS = 16
 N_FIRST = 2
 EXP_SCALE = DH ** (-0.5) * math.log2(math.e)
-FAR_CHUNK = 256
+SLABS = 4
 VMEM_LIMIT = 57 * 1024 * 1024
 MESH = pl.DeviceIdType.MESH
 FROM_PARTNER, FROM_BEHIND, RELAYED = 0, 1, 2
@@ -59,7 +59,7 @@
 def kernel(
     rows, cols,
     q_hbm, k_hbm, v_hbm, wmk_hbm, wmv_hbm, wfk_hbm, wfv_hbm, out_ref,
-    q_ref, k_ref, v_ref, wmk_ref, wmv_ref, wfk_ref, wfv_ref, fetch_sem,
+    q_ref, kv_ref, wmk_ref, wmv_ref, wfk_ref, wfv_ref, fetch_sem,
     wide, mid_buf, far_buf, near, top_ref, den_ref, acc_ref, rest_ref,
     far_top, far_den, far_acc,
     near_send, near_recv, mid_send, mid_recv, pass_send, pass_recv,
@@ -90,7 +90,7 @@
     fetches = [
         fetch(i, src, dst)
         for i, (src, dst) in enumerate((
-            (k_hbm, k_ref), (v_hbm, v_ref), (wfk_hbm, wfk_ref), (wfv_hbm, wfv_ref),
+            (k_hbm, kv_ref.at[0]), (v_hbm, kv_ref.at[1]), (wfk_hbm, wfk_ref), (wfv_hbm, wfv_ref),
             (wmk_hbm, wmk_ref), (wmv_hbm, wmv_ref), (q_hbm, q_ref),
         ))
     ]
@@ -175,7 +175,7 @@
         return same(far_buf.at[2 * r + side], down_send.at[r], down_recv.at[r], (row + 2, col))
 
     def cross(r):
-        return same(far_buf.at[2 * r + side], cross_send.at[r], cross_recv.at[r], beside)
+        return same(far_buf.at[2 * r + side], cross_send.at[lax.rem(r, 2)], cross_recv.at[lax.rem(r, 2)], beside)
 
     def lift(r):
         return same(far_buf.at[2 * r + side], lift_send.at[r], lift_recv.at[r], (row, col + 2))
@@ -192,43 +192,36 @@
     def mid_pass(p, s):
         return same(mid_span(2 * p + s), pass_send.at[p], pass_recv.at[p], partner)
 
-    def near_copy(i, half):
+    def near_copy(half):
         lanes = pl.ds(pl.multiple_of(half * (KV // 2), KV // 2), KV // 2)
         return remote(
-            own[i].at[:, lanes], near.at[FROM_PARTNER, i, :, lanes],
-            near_send.at[FROM_PARTNER, i, half], near_recv.at[FROM_PARTNER, i, half], partner,
+            kv_ref.at[:, :, lanes], near.at[FROM_PARTNER, :, :, lanes],
+            near_send.at[FROM_PARTNER, half], near_recv.at[FROM_PARTNER, half], partner,
         )
 
-    def halves(f):
-        for half in range(2):
-            for i in range(2):
-                f(near_copy(i, half))
-
-    def behind_copy(i, h):
+    def behind_copy(h):
         lanes = head_lanes(h)
         return remote(
-            own[i].at[:, lanes], near.at[FROM_BEHIND, i, :, lanes],
-            near_send.at[FROM_BEHIND, i, h], near_recv.at[FROM_BEHIND, i, h], ahead,
+            kv_ref.at[:, :, lanes], near.at[FROM_BEHIND, :, :, lanes],
+            near_send.at[FROM_BEHIND, h], near_recv.at[FROM_BEHIND, h], ahead,
         )
 
-    def relay_copy(i, h):
+    def relay_copy(h):
         lanes = head_lanes(h)
         return remote(
-            near.at[FROM_BEHIND, i, :, lanes], near.at[RELAYED, i, :, lanes],
-            near_send.at[RELAYED, i, h], near_recv.at[RELAYED, i, h], partner,
+            near.at[FROM_BEHIND, :, :, lanes], near.at[RELAYED, :, :, lanes],
+            near_send.at[RELAYED, h], near_recv.at[RELAYED, h], partner,
         )
 
     def behind_start(h):
-        for i in range(2):
-            behind_copy(i, h).start()
-
-    own = (k_ref, v_ref)
+        behind_copy(h).start()
+
     mid_rows = pl.ds(pl.multiple_of(col * mids, mids), mids)
     far_rows = pl.ds(pl.multiple_of(pair * fars, fars), fars)
 
-    def spread_out(s, src):
+    def spread_out(s):
         for h in range(HK):
-            wide[s * HK + h] = src[:, h * DH:(h + 1) * DH].astype(jnp.float32)
+            wide[s * HK + h] = kv_ref[s, :, h * DH:(h + 1) * DH].astype(jnp.float32)
 
     def summarise(s, squeeze, weight):
         count = tok // squeeze
@@ -267,8 +260,8 @@
 
     for copy in fetches[:2]:
         copy.wait()
-    spread_out(0, k_ref)
-    spread_out(1, v_ref)
+    spread_out(0)
+    spread_out(1)
     for copy in fetches[2:4]:
         copy.wait()
     summarise(0, FAR, wfk_ref)
@@ -276,7 +269,7 @@
     pl.semaphore_wait(barrier, greeted)
     others(lambda p: swap(p, pair).start())
     side_swap(row, pair).start()
-    when(side == 0, lambda: halves(lambda copy: copy.start()))
+    when(side == 0, lambda: loop(0, 2, lambda half: near_copy(half).start()))
     for copy in fetches[4:6]:
         copy.wait()
     summarise(0, MID, wmk_ref)
@@ -285,6 +278,7 @@
     when(side == 0, lambda: mid_pass(pair, 0).start())
 
     sends = pos + 2 < total
+    starts = feeds_beside & (side == 0)
     n_first = jnp.where(is_hub, N_FIRST, HK)
 
     fetches[6].wait()
@@ -300,11 +294,10 @@
             seen = iota((tok, tok), 0) <= iota((tok, tok), 1)
             work = []
             if with_partner:
-                near_copy(0, i).wait_recv()
-                near_copy(1, i).wait_recv()
+                near_copy(i).wait_recv()
             for h in (2 * i, 2 * i + 1):
-                keys = [k_ref[:, head_lanes(h)]]
-                flats = [flat(v_ref[:, head_lanes(h)])]
+                keys = [kv_ref[0, :, head_lanes(h)]]
+                flats = [flat(kv_ref[1, :, head_lanes(h)])]
                 if with_partner:
                     keys.append(near[FROM_PARTNER, 0, :, head_lanes(h)])
                     flats.append(flat(near[FROM_PARTNER, 1, :, head_lanes(h)]))
@@ -325,6 +318,7 @@
         when(low == 1, lambda: twin(row - 1, side).start())
 
     def near_more():
+        when(sends & starts, lambda: loop(0, HK, behind_start))
         side_swap(other_row, pair).wait_recv()
         loop(pair + 1, pairs, lambda p: up(p).start())
 
@@ -334,7 +328,7 @@
 
         loop(pair + 1, pairs, over)
         loop(0, pair, lambda p: swap(p, p).wait_recv())
-        when(sends, lambda: loop(0, n_first, behind_start))
+        when(sends & jnp.logical_not(starts), lambda: loop(0, n_first, behind_start))
         when(jnp.logical_not(is_last), lambda: down(row).start())
 
     def near_own(with_partner):
@@ -410,13 +404,11 @@
         loop(0, 2, one)
 
     def arrive(h):
-        for i in range(2):
-            behind_copy(i, h).wait_recv()
-            relay_copy(i, h).start()
+        behind_copy(h).wait_recv()
+        relay_copy(h).start()
 
     def near_last(h):
-        for i in range(2):
-            relay_copy(i, h).wait_recv()
+        relay_copy(h).wait_recv()
         slots = (FROM_BEHIND, RELAYED)
         keys = [near[slot, 0, :, head_lanes(h)] for slot in slots]
         flats = [flat(near[slot, 1, :, head_lanes(h)]) for slot in slots]
@@ -431,13 +423,12 @@
             acc_ref[n] = acc_ref[n] * fade + acc
 
     line = far_buf.shape[1]
-    per = max(1, min(2 * rows, FAR_CHUNK // line))
     def far_chunk(j):
         def part(h, base):
-            block = far_buf[pl.ds(j * per, per), :, head_lanes(h, base)]
-            return block.reshape(per * line, DH)
-
-        seen = iota((per * line, 1), 0) + j * (per * line) < 2 * row * line
+            block = far_buf[pl.ds(j * SLABS, SLABS), :, head_lanes(h, base)]
+            return block.reshape(SLABS * line, DH)
+
+        seen = iota((SLABS * line, 1), 0) + j * (SLABS * line) < 2 * row * line
         work = []
         for h in range(HK):
             keys, flats = part(h, 0), flat(part(h, KV))
@@ -452,12 +443,12 @@
             far_den[n] = far_den[n] * fade + den
             far_acc[n] = far_acc[n] * fade + acc
 
-    row_span = per // 2
-    newest = (row + row_span - 1) // row_span - 1
-
-    def far_chunks(name, low_chunk, high_chunk):
-        loop(low_chunk * row_span, jnp.minimum(high_chunk * row_span, row), lambda r: twin(r, 1 - side).wait_recv())
-        loop(low_chunk, high_chunk, far_chunk)
+    def far_rows(j):
+        loop(2 * j, jnp.minimum(2 * j + 2, row), lambda r: twin(r, 1 - side).wait_recv())
+        far_chunk(j)
+
+    def far_back(k_low, k_high):
+        loop(k_low, k_high, lambda k: far_rows(high - 1 - k))
 
     def finish(with_far, h):
         for g in range(GROUP):
@@ -477,7 +468,7 @@
 
         @pl.when(side == 0)
         def _():
-            halves(lambda copy: copy.wait_send())
+            loop(0, 2, lambda half: near_copy(half).wait_send())
             mid_pass(pair, 0).wait_send()
 
     def feeds_next_done():
@@ -501,43 +492,40 @@
         def _():
             near_last(h)
 
-    def far_newest():
-        far_chunks("FAR1", newest, newest + 1)
-
-    def far_rest():
-        far_chunks("FAR2", 0, newest)
-
     plain = jnp.logical_not(is_hub)
-    far_first = (low == 0) & (pair == 0)
+    near_late = (low == 0) & (pair == 0) & (side == 0) & (high > 1)
+    far_late = (low == 0) & (pair == 0) & (high > 1) & jnp.logical_not(is_last)
 
     def step(s):
         when((s == 0) & (high > 0) & plain, lambda: hand_on(0))
         when((s < HK) & (s != 2), lambda: near_in(s))
-        when((s == 1) & plain & (high > 1), lambda: hand_on(1))
+        when(s == 0, lambda: far_back(jnp.where(low == 1, -1, 0), jnp.where(plain & jnp.logical_not(far_late), jnp.minimum(high, 1), 0)))
+        when((s == 1) & (high > 1) & plain, lambda: hand_on(1))
         when(s > 0, lambda: near_end(s - 1))
 
         @pl.when(s == 2)
         def _():
             loop(jnp.where(is_hub, 0, 2), jnp.where(is_hub, jnp.minimum(high, 1), high), hand_on)
-
-            def far(i):
-                when((i == 0) != far_first, lambda: near_in(2))
-                when((row > 0) & (i == 0), far_newest)
-
-            loop(0, 2, far)
-            when((row > 0) & plain, far_rest)
+            when(jnp.logical_not(near_late), lambda: near_in(2))
+            far_back(jnp.where(plain & jnp.logical_not(far_late), 1, 0), jnp.where(plain, high, jnp.minimum(high, 1)))
+            when(near_late, lambda: near_in(2))
+            when((row > 0) & plain, lambda: loop(0, 2, functools.partial(finish, True)))
 
         @pl.when(s == HK - 1)
         def _():
             sent_early()
-            when(is_hub, lambda: loop(1, high, hand_on))
-            when(plain & (row > 0), lambda: loop(0, HK - 1, functools.partial(finish, True)))
+            when(is_hub & (high > 1), lambda: hand_on(1))
+            when(plain & (row > 0), lambda: loop(2, HK - 1, functools.partial(finish, True)))
 
     loop(0, HK + 1, step)
 
     @pl.when(row > 0)
     def _():
-        when(is_hub, far_rest)
+        @pl.when(is_hub)
+        def _():
+            loop(2, high, hand_on)
+            far_back(1, high)
+
         loop(jnp.where(is_hub, 0, HK - 1), HK, functools.partial(finish, True))
 
     @pl.when(row == 0)
@@ -549,13 +537,11 @@
 
     @pl.when(pos + 2 < total)
     def _():
-        for i in range(2):
-            loop(0, HK, lambda h, i=i: behind_copy(i, h).wait_send())
+        loop(0, HK, lambda h: behind_copy(h).wait_send())
 
     @pl.when(pos >= 2)
     def _():
-        for i in range(2):
-            loop(0, HK, lambda h, i=i: relay_copy(i, h).wait_send())
+        loop(0, HK, lambda h: relay_copy(h).wait_send())
 
 
 def body(rows, cols, queries, keys, values, *weights):
@@ -571,7 +557,9 @@
         in_specs=[pl.BlockSpec(memory_space=pltpu.HBM)] * 7,
         out_specs=vmem,
         scratch_shapes=[
-            *[pltpu.VMEM(a.shape, a.dtype) for a in (queries, keys, values, *weights)],
+            pltpu.VMEM(queries.shape, bf16),
+            pltpu.VMEM((2, *keys.shape), bf16),
+            *[pltpu.VMEM(a.shape, a.dtype) for a in weights],
             dma((7,)),
             pltpu.VMEM((2 * HK, tok, DH), f32),
             pltpu.VMEM((cols * (tok // MID), 2 * KV), bf16),
@@ -584,10 +572,13 @@
             pltpu.VMEM((HQ, 1, tok), f32),
             pltpu.VMEM((HQ, 1, tok), f32),
             pltpu.VMEM((HQ, DH, tok), f32),
-            dma((3, 2, HK)),
-            dma((3, 2, HK)),
+            dma((3, HK)),
+            dma((3, HK)),
             *[dma((pairs,))] * 9,
-            *[dma((rows,))] * 8,
+            *[dma((rows,))] * 2,
+            *[dma((2,))] * 2,
+            *[dma((max(rows - 6, 1),))] * 2,
+            *[dma((rows,))] * 2,
         ],
         compiler_params=pltpu.CompilerParams(
             collective_id=0, has_side_effects=True, vmem_limit_bytes=VMEM_LIMIT

time: 26.7 us -> 25.7 us (0.963)
  Pallas kernels: 25.5 us -> 24.3 us
    pallas_call x1, Pallas kernels: 25.5 us -> 24.3 us  [body(): pl.pallas_call(functools.partial(kernel, rows, cols), out_shape=pltpu.VME...]
where the time goes in v4:
time: 25.7 us; the launch traced here: 25.3 us
  Pallas kernels  24.3 us (95%)
  local copies, waits for them, and re-layouts  0.97 us (4%)
    pallas_call x1, Pallas kernels, body(): pl.pallas_call(functools.partial(kernel, rows, cols), out_shape=pltpu.VME...  24.3 us
    unnamed x1, local copies, waits for them, and re-layouts  0.97 us

profile of v4, /device:TPU:31, one launch (start us, length us, event | category | flops | bytes accessed | tf_op | source)
XLA Modules:
  0.0 25.3 jit_solution(12128097988728399013)
XLA Ops:
  0.0 24.3 %shard_map.73 = bf16[256,2048]{1,0:T(8,128)(2,1)S(1)} custom-call(bf16[256,2048]{1,0:T(8,128)(2,1)} %q_hbm.1, bf16[256,512]{1,0:T(8,128)(2,1)} %k_hbm.1, bf16[256,512]{1,0:T(8,128)(2,1)} %v_hbm.1, bf16[1024,128]{1,0:T(8,128)(2,1)} %wmk_hbm.1, bf16[1024,128]{1,0:T(8,128)(2,1)} %wmv_hbm.1, bf16[2048,128]{1,0:T(8,128)(2,1)} %wfk_hbm.1, bf16[2048,128]{1,0:T(8,128)(2,1)} %wfv_hbm.1), custom_call_target="tpu_custom_call" | custom-call | tf_op jit(solution)/shard_map/pallas_call | solution.py:554
  24.4 1.0 %copy.9 = bf16[256,2048]{1,0:T(8,128)(2,1)} copy(bf16[256,2048]{1,0:T(8,128)(2,1)S(1)} %shard_map.73) | data formatting | bytes 2097152

commit v5 on v4

--- a/solution.py
+++ b/solution.py
@@ -24,7 +24,7 @@
 SLABS = 4
 VMEM_LIMIT = 57 * 1024 * 1024
 MESH = pl.DeviceIdType.MESH
-FROM_PARTNER, FROM_BEHIND, RELAYED = 0, 1, 2
+FROM_BEHIND, RELAYED, FROM_PARTNER = 0, 1, 2
 
 
 def score(k, q):
@@ -62,9 +62,9 @@
     q_ref, kv_ref, wmk_ref, wmv_ref, wfk_ref, wfv_ref, fetch_sem,
     wide, mid_buf, far_buf, near, top_ref, den_ref, acc_ref, rest_ref,
     far_top, far_den, far_acc,
-    near_send, near_recv, mid_send, mid_recv, pass_send, pass_recv,
-    swap_send, swap_recv, side_send, side_recv, up_send,
-    down_send, down_recv, cross_send, cross_recv, lift_send, lift_recv, twin_send, twin_recv,
+    near_send, near_recv, own_sem, mid_sem, pass_send, pass_recv,
+    swap_send, swap_recv, side_send, side_recv,
+    down_send, down_recv, cross_send, lift_send, twin_send, twin_recv,
 ):
     tok = q_ref.shape[0]
     mids, fars = tok // MID, tok // FAR
@@ -169,16 +169,16 @@
         return same(far_block(r, p), side_send.at[p], side_recv.at[p], beside)
 
     def up(p):
-        return same(far_block(other_row, pair), up_send.at[p], side_recv.at[pair], (row, 2 * p + side))
+        return same(far_block(other_row, pair), pass_send.at[p], side_recv.at[pair], (row, 2 * p + side))
 
     def down(r):
         return same(far_buf.at[2 * r + side], down_send.at[r], down_recv.at[r], (row + 2, col))
 
     def cross(r):
-        return same(far_buf.at[2 * r + side], cross_send.at[lax.rem(r, 2)], cross_recv.at[lax.rem(r, 2)], beside)
+        return same(far_buf.at[2 * r + side], cross_send.at[lax.rem(r, 2)], down_recv.at[r], beside)
 
     def lift(r):
-        return same(far_buf.at[2 * r + side], lift_send.at[r], lift_recv.at[r], (row, col + 2))
+        return same(far_buf.at[2 * r + side], lift_send.at[r], down_recv.at[r], (row, col + 2))
 
     def twin(r, s):
         return same(far_buf.at[2 * r + s], twin_send.at[r], twin_recv.at[r], partner)
@@ -187,7 +187,7 @@
         return mid_buf.at[pl.ds(pl.multiple_of(c * mids, mids), mids), :]
 
     def mid_copy(p_to, p_from):
-        return same(mid_span(2 * p_from + side), mid_send.at[p_to], mid_recv.at[p_from], (row, 2 * p_to + side))
+        return same(mid_span(2 * p_from + side), mid_sem.at[p_to], mid_sem.at[p_from], (row, 2 * p_to + side))
 
     def mid_pass(p, s):
         return same(mid_span(2 * p + s), pass_send.at[p], pass_recv.at[p], partner)
@@ -196,7 +196,7 @@
         lanes = pl.ds(pl.multiple_of(half * (KV // 2), KV // 2), KV // 2)
         return remote(
             kv_ref.at[:, :, lanes], near.at[FROM_PARTNER, :, :, lanes],
-            near_send.at[FROM_PARTNER, half], near_recv.at[FROM_PARTNER, half], partner,
+            own_sem.at[half], own_sem.at[half], partner,
         )
 
     def behind_copy(h):
@@ -278,7 +278,11 @@
     when(side == 0, lambda: mid_pass(pair, 0).start())
 
     sends = pos + 2 < total
-    starts = feeds_beside & (side == 0)
+    n_now = (
+        jnp.where(feeds_beside & (side == 0), HK, 0)
+        + jnp.where((side == 0) & (low == 1) & (pair == pairs - 2), 1, 0)
+        + jnp.where(is_hub & (side == 1), 1, 0)
+    )
     n_first = jnp.where(is_hub, N_FIRST, HK)
 
     fetches[6].wait()
@@ -318,7 +322,7 @@
         when(low == 1, lambda: twin(row - 1, side).start())
 
     def near_more():
-        when(sends & starts, lambda: loop(0, HK, behind_start))
+        when(sends, lambda: loop(0, n_now, behind_start))
         side_swap(other_row, pair).wait_recv()
         loop(pair + 1, pairs, lambda p: up(p).start())
 
@@ -328,7 +332,7 @@
 
         loop(pair + 1, pairs, over)
         loop(0, pair, lambda p: swap(p, p).wait_recv())
-        when(sends & jnp.logical_not(starts), lambda: loop(0, n_first, behind_start))
+        when(sends, lambda: loop(n_now, n_first, behind_start))
         when(jnp.logical_not(is_last), lambda: down(row).start())
 
     def near_own(with_partner):
@@ -423,7 +427,11 @@
             acc_ref[n] = acc_ref[n] * fade + acc
 
     line = far_buf.shape[1]
-    def far_chunk(j):
+    def put(n, whole):
+        lanes = pl.ds(pl.multiple_of(n * DH, DH), DH)
+        out_ref[:, lanes] = whole.astype(out_ref.dtype).T
+
+    def far_chunk(j, last=False):
         def part(h, base):
             block = far_buf[pl.ds(j * SLABS, SLABS), :, head_lanes(h, base)]
             return block.reshape(SLABS * line, DH)
@@ -439,13 +447,15 @@
             top = jnp.maximum(before, top_of([s]))
             fade = powers(before, top)
             den, acc = weigh([s], top, [flats])
-            far_top[n] = top
-            far_den[n] = far_den[n] * fade + den
-            far_acc[n] = far_acc[n] * fade + acc
-
-    def far_rows(j):
+            den, acc = far_den[n] * fade + den, far_acc[n] * fade + acc
+            if last:
+                put(n, acc_ref[n] * inverse(den_ref[n]) + rest_ref[n] + acc * inverse(den))
+            else:
+                far_top[n], far_den[n], far_acc[n] = top, den, acc
+
+    def far_rows(j, last=False):
         loop(2 * j, jnp.minimum(2 * j + 2, row), lambda r: twin(r, 1 - side).wait_recv())
-        far_chunk(j)
+        far_chunk(j, last)
 
     def far_back(k_low, k_high):
         loop(k_low, k_high, lambda k: far_rows(high - 1 - k))
@@ -456,8 +466,7 @@
             whole = acc_ref[n] * inverse(den_ref[n]) + rest_ref[n]
             if with_far:
                 whole = whole + far_acc[n] * inverse(far_den[n])
-            lanes = pl.ds(pl.multiple_of(n * DH, DH), DH)
-            out_ref[:, lanes] = whole.astype(out_ref.dtype).T
+            put(n, whole)
 
     def sent_early():
         others(lambda p: swap(p, pair).wait_send())
@@ -506,9 +515,11 @@
         @pl.when(s == 2)
         def _():
             loop(jnp.where(is_hub, 0, 2), jnp.where(is_hub, jnp.minimum(high, 1), high), hand_on)
-            when(jnp.logical_not(near_late), lambda: near_in(2))
-            far_back(jnp.where(plain & jnp.logical_not(far_late), 1, 0), jnp.where(plain, high, jnp.minimum(high, 1)))
-            when(near_late, lambda: near_in(2))
+            first = jnp.where(plain & jnp.logical_not(far_late), 1, 0)
+            split = jnp.where(near_late, first + 1, first)
+            far_back(first, split)
+            near_in(2)
+            far_back(split, jnp.where(plain, high, jnp.minimum(high, 1)))
             when((row > 0) & plain, lambda: loop(0, 2, functools.partial(finish, True)))
 
         @pl.when(s == HK - 1)
@@ -521,12 +532,17 @@
 
     @pl.when(row > 0)
     def _():
-        @pl.when(is_hub)
+        ends_far = is_hub & (high > 1)
+
+        @pl.when(ends_far)
         def _():
             loop(2, high, hand_on)
-            far_back(1, high)
-
-        loop(jnp.where(is_hub, 0, HK - 1), HK, functools.partial(finish, True))
+            far_back(1, high - 1)
+            far_rows(0, True)
+
+        @pl.when(jnp.logical_not(ends_far))
+        def _():
+            loop(jnp.where(is_hub, 0, HK - 1), HK, functools.partial(finish, True))
 
     @pl.when(row == 0)
     def _():
@@ -572,12 +588,13 @@
             pltpu.VMEM((HQ, 1, tok), f32),
             pltpu.VMEM((HQ, 1, tok), f32),
             pltpu.VMEM((HQ, DH, tok), f32),
-            dma((3, HK)),
-            dma((3, HK)),
-            *[dma((pairs,))] * 9,
+            dma((2, HK)),
+            dma((2, HK)),
+            dma((2,)),
+            *[dma((pairs,))] * 7,
             *[dma((rows,))] * 2,
-            *[dma((2,))] * 2,
-            *[dma((max(rows - 6, 1),))] * 2,
+            dma((2,)),
+            dma((max(rows - 6, 1),)),
             *[dma((rows,))] * 2,
         ],
         compiler_params=pltpu.CompilerParams(

time: 25.7 us -> 27.7 us (1.078)
  Pallas kernels: 24.3 us -> 26.6 us
    pallas_call x1, Pallas kernels: 24.3 us -> 26.6 us  [body(): pl.pallas_call(functools.partial(kernel, rows, cols), out_shape=pltpu.VME...]
where the time goes in v5:
time: 27.7 us; the launch traced here: 27.5 us
  Pallas kernels  26.6 us (96%)
  local copies, waits for them, and re-layouts  0.97 us (4%)
    pallas_call x1, Pallas kernels, body(): pl.pallas_call(functools.partial(kernel, rows, cols), out_shape=pltpu.VME...  26.6 us
    unnamed x1, local copies, waits for them, and re-layouts  0.97 us

profile of v5, /device:TPU:31, one launch (start us, length us, event | category | flops | bytes accessed | tf_op | source)
XLA Modules:
  0.0 27.5 jit_solution(1502841210970531364)
XLA Ops:
  0.0 26.6 %shard_map.73 = bf16[256,2048]{1,0:T(8,128)(2,1)S(1)} custom-call(bf16[256,2048]{1,0:T(8,128)(2,1)} %q_hbm.1, bf16[256,512]{1,0:T(8,128)(2,1)} %k_hbm.1, bf16[256,512]{1,0:T(8,128)(2,1)} %v_hbm.1, bf16[1024,128]{1,0:T(8,128)(2,1)} %wmk_hbm.1, bf16[1024,128]{1,0:T(8,128)(2,1)} %wmv_hbm.1, bf16[2048,128]{1,0:T(8,128)(2,1)} %wfk_hbm.1, bf16[2048,128]{1,0:T(8,128)(2,1)} %wfv_hbm.1), custom_call_target="tpu_custom_call" | custom-call | tf_op jit(solution)/shard_map/pallas_call | solution.py:570
  26.6 1.0 %copy.9 = bf16[256,2048]{1,0:T(8,128)(2,1)} copy(bf16[256,2048]{1,0:T(8,128)(2,1)S(1)} %shard_map.73) | data formatting | bytes 2097152

commit v6 on v5

--- a/solution.py
+++ b/solution.py
@@ -278,11 +278,7 @@
     when(side == 0, lambda: mid_pass(pair, 0).start())
 
     sends = pos + 2 < total
-    n_now = (
-        jnp.where(feeds_beside & (side == 0), HK, 0)
-        + jnp.where((side == 0) & (low == 1) & (pair == pairs - 2), 1, 0)
-        + jnp.where(is_hub & (side == 1), 1, 0)
-    )
+    starts = feeds_beside & (side == 0)
     n_first = jnp.where(is_hub, N_FIRST, HK)
 
     fetches[6].wait()
@@ -322,7 +318,7 @@
         when(low == 1, lambda: twin(row - 1, side).start())
 
     def near_more():
-        when(sends, lambda: loop(0, n_now, behind_start))
+        when(sends & starts, lambda: loop(0, HK, behind_start))
         side_swap(other_row, pair).wait_recv()
         loop(pair + 1, pairs, lambda p: up(p).start())
 
@@ -332,7 +328,7 @@
 
         loop(pair + 1, pairs, over)
         loop(0, pair, lambda p: swap(p, p).wait_recv())
-        when(sends, lambda: loop(n_now, n_first, behind_start))
+        when(sends & jnp.logical_not(starts), lambda: loop(0, n_first, behind_start))
         when(jnp.logical_not(is_last), lambda: down(row).start())
 
     def near_own(with_partner):

time: 27.7 us -> 25.3 us (0.913)
  Pallas kernels: 26.6 us -> 24.1 us
    pallas_call x1, Pallas kernels: 26.6 us -> 24.1 us  [body(): pl.pallas_call(functools.partial(kernel, rows, cols), out_shape=pltpu.VME...]
where the time goes in v6:
time: 25.3 us; the launch traced here: 25 us
  Pallas kernels  24.1 us (95%)
  local copies, waits for them, and re-layouts  0.97 us (4%)
    pallas_call x1, Pallas kernels, body(): pl.pallas_call(functools.partial(kernel, rows, cols), out_shape=pltpu.VME...  24.1 us
    unnamed x1, local copies, waits for them, and re-layouts  0.97 us

profile of v6, /device:TPU:31, one launch (start us, length us, event | category | flops | bytes accessed | tf_op | source)
XLA Modules:
  0.0 25.0 jit_solution(14539920667126273592)
XLA Ops:
  0.0 24.1 %shard_map.73 = bf16[256,2048]{1,0:T(8,128)(2,1)S(1)} custom-call(bf16[256,2048]{1,0:T(8,128)(2,1)} %q_hbm.1, bf16[256,512]{1,0:T(8,128)(2,1)} %k_hbm.1, bf16[256,512]{1,0:T(8,128)(2,1)} %v_hbm.1, bf16[1024,128]{1,0:T(8,128)(2,1)} %wmk_hbm.1, bf16[1024,128]{1,0:T(8,128)(2,1)} %wmv_hbm.1, bf16[2048,128]{1,0:T(8,128)(2,1)} %wfk_hbm.1, bf16[2048,128]{1,0:T(8,128)(2,1)} %wfv_hbm.1), custom_call_target="tpu_custom_call" | custom-call | tf_op jit(solution)/shard_map/pallas_call | solution.py:566
  24.1 1.0 %copy.9 = bf16[256,2048]{1,0:T(8,128)(2,1)} copy(bf16[256,2048]{1,0:T(8,128)(2,1)S(1)} %shard_map.73) | data formatting | bytes 2097152

commit v7 on v6

--- a/solution.py
+++ b/solution.py
@@ -407,7 +407,7 @@
         behind_copy(h).wait_recv()
         relay_copy(h).start()
 
-    def near_last(h):
+    def near_last(h, last=False):
         relay_copy(h).wait_recv()
         slots = (FROM_BEHIND, RELAYED)
         keys = [near[slot, 0, :, head_lanes(h)] for slot in slots]
@@ -419,8 +419,11 @@
             top = jnp.maximum(before, top_of(parts))
             den, acc = weigh(parts, top, flats)
             fade = powers(before, top)
-            den_ref[n] = den_ref[n] * fade + den
-            acc_ref[n] = acc_ref[n] * fade + acc
+            den, acc = den_ref[n] * fade + den, acc_ref[n] * fade + acc
+            if last:
+                put(n, acc * inverse(den) + rest_ref[n] + far_acc[n] * inverse(far_den[n]))
+            else:
+                den_ref[n], acc_ref[n] = den, acc
 
     line = far_buf.shape[1]
     def put(n, whole):
@@ -501,12 +504,14 @@
     near_late = (low == 0) & (pair == 0) & (side == 0) & (high > 1)
     far_late = (low == 0) & (pair == 0) & (high > 1) & jnp.logical_not(is_last)
 
+    ends_near = plain & (row > 0)
+
     def step(s):
         when((s == 0) & (high > 0) & plain, lambda: hand_on(0))
         when((s < HK) & (s != 2), lambda: near_in(s))
         when(s == 0, lambda: far_back(jnp.where(low == 1, -1, 0), jnp.where(plain & jnp.logical_not(far_late), jnp.minimum(high, 1), 0)))
         when((s == 1) & (high > 1) & plain, lambda: hand_on(1))
-        when(s > 0, lambda: near_end(s - 1))
+        when((s > 0) & jnp.logical_not(ends_near & (s == HK)), lambda: near_end(s - 1))
 
         @pl.when(s == 2)
         def _():
@@ -525,6 +530,7 @@
             when(plain & (row > 0), lambda: loop(2, HK - 1, functools.partial(finish, True)))
 
     loop(0, HK + 1, step)
+    when(ends_near, lambda: near_last(HK - 1, True))
 
     @pl.when(row > 0)
     def _():
@@ -536,9 +542,9 @@
             far_back(1, high - 1)
             far_rows(0, True)
 
-        @pl.when(jnp.logical_not(ends_far))
-        def _():
-            loop(jnp.where(is_hub, 0, HK - 1), HK, functools.partial(finish, True))
+        @pl.when(is_hub & jnp.logical_not(ends_far))
+        def _():
+            loop(0, HK, functools.partial(finish, True))
 
     @pl.when(row == 0)
     def _():

time: 25.3 us -> 25.2 us (level)
  no operation moved by 1% of the time
where the time goes in v7:
time: 25.2 us; the launch traced here: 25 us
  Pallas kernels  24 us (95%)
  local copies, waits for them, and re-layouts  0.97 us (4%)
    pallas_call x1, Pallas kernels, body(): pl.pallas_call(functools.partial(kernel, rows, cols), out_shape=pltpu.VME...  24 us
    unnamed x1, local copies, waits for them, and re-layouts  0.97 us

profile of v7, /device:TPU:31, one launch (start us, length us, event | category | flops | bytes accessed | tf_op | source)
XLA Modules:
  0.0 25.0 jit_solution(5158777301053807581)
XLA Ops:
  0.0 24.0 %shard_map.73 = bf16[256,2048]{1,0:T(8,128)(2,1)S(1)} custom-call(bf16[256,2048]{1,0:T(8,128)(2,1)} %q_hbm.1, bf16[256,512]{1,0:T(8,128)(2,1)} %k_hbm.1, bf16[256,512]{1,0:T(8,128)(2,1)} %v_hbm.1, bf16[1024,128]{1,0:T(8,128)(2,1)} %wmk_hbm.1, bf16[1024,128]{1,0:T(8,128)(2,1)} %wmv_hbm.1, bf16[2048,128]{1,0:T(8,128)(2,1)} %wfk_hbm.1, bf16[2048,128]{1,0:T(8,128)(2,1)} %wfv_hbm.1), custom_call_target="tpu_custom_call" | custom-call | tf_op jit(solution)/shard_map/pallas_call | solution.py:572
  24.0 1.0 %copy.9 = bf16[256,2048]{1,0:T(8,128)(2,1)} copy(bf16[256,2048]{1,0:T(8,128)(2,1)S(1)} %shard_map.73) | data formatting | bytes 2097152
